TPU v7x, 128 devices: a whole 4x4x4 slice. The times are simulated.
128 devices in a mesh: probe: 4 (over z_hi, core), fsdp: 32 (over y, z_lo, x).
Axes of the slice: x: 4, y: 4, z: 4 (z_hi: 2, z_lo: 2; z = z_hi * 2 + z_lo), core: 2. Of those that a mesh axis runs over, the one named last changes fastest.
Arguments:
- hidden: bfloat16 [65536, 2048], P(('probe', 'fsdp')), may hold values from -6 to 6
- norm_gain: bfloat16 [2048], replicated, may hold values from 0.5 to 1.5
- query_weight: bfloat16 [2048, 2048], P('fsdp'), may hold values from -1 to 1
- key_weight: bfloat16 [2048, 512], P('fsdp'), may hold values from -16 to 16
- value_weight: bfloat16 [2048, 512], P('fsdp'), may hold values from -0.125 to 0.125
- output_weight: bfloat16 [2048, 2048], P('fsdp'), may hold values from -0.125 to 0.125
- probe_seed: int32 [4], P('probe'), may hold values from 0 to 1073741823
Outputs:
- curvature_value: float32 [2048, 512], P('fsdp', 'probe')
- curvature_output: float32 [2048, 2048], P('fsdp', 'probe')
All inputs are finite; a program needn't handle non-finite values.
Results may differ from a plain program's by a relative error of at most 0.024.
Values may be sent and summed in bfloat16 or wider, within the bound.
A program may use at most 128 MiB of HBM per device.

v0:
```python
import jax
import jax.numpy as jnp
from jax import lax
from jax.sharding import PartitionSpec as P

HEAD_DIM = 128
SEQ = 256


norm_eps = 1e-05
rope_base = 500000.0


def in_one_piece(arrays, axis, dim, along):
    both = jnp.concatenate(arrays, axis=along)
    result, at, finished = (lax.all_gather(both, axis, axis=dim, tiled=True), 0, [])
    for a in arrays:
        finished.append(lax.slice_in_dim(result, at, at + a.shape[along], axis=along))
        at += a.shape[along]
    return tuple(finished)


def split_up(value, dim, size):
    dims = value.shape
    parts = value.reshape(*dims[:dim], size, dims[dim] // size, *dims[dim + 1 :])
    return jnp.moveaxis(parts, dim, 0)


def sent_and_summed(value, axis, dim):
    size = lax.axis_size(axis)
    parts = lax.all_to_all(split_up(value, dim, size), axis, 0, 0, tiled=True)
    return jnp.sum(parts.astype(jnp.float32), axis=0)


def sign_table(seed_value, matrix_code, row_total, column_total):
    row_index = lax.broadcasted_iota(jnp.int32, (row_total, column_total), 0)
    column_index = lax.broadcasted_iota(jnp.int32, (row_total, column_total), 1)
    hashed = (row_index * column_total + column_index) * 747796405 + (
        seed_value * 1664525 + matrix_code * 374761393
    )
    hashed = hashed ^ lax.shift_right_logical(hashed, jnp.int32(15))
    hashed = hashed * 668265261
    hashed = hashed ^ lax.shift_right_logical(hashed, jnp.int32(13))
    hashed = hashed * 1274126177
    hashed = hashed ^ lax.shift_right_logical(hashed, jnp.int32(16))
    return jnp.where(hashed & 1 == 1, 1.0, -1.0).astype(jnp.bfloat16)


def normalize(rows_in, gain_row):
    values = rows_in.astype(jnp.float32)
    inverse = lax.rsqrt(jnp.mean(values * values, axis=1, keepdims=True) + norm_eps)
    return (values * inverse * gain_row.astype(jnp.float32)[None, :]).astype(jnp.bfloat16)


def rotate(projected, head_count):
    row_count = projected.shape[0]
    columns = projected.shape[1]
    head_size = columns // head_count
    half_dim = head_size // 2
    position = (lax.broadcasted_iota(jnp.int32, (row_count, 1), 0) % SEQ).astype(jnp.float32)
    exponent = lax.broadcasted_iota(jnp.int32, (1, half_dim), 1).astype(jnp.float32) * (
        -2.0 / head_size
    )
    frequency = jnp.power(jnp.float32(rope_base), exponent)
    angles = position * frequency
    cosine = jnp.cos(angles)[:, None, :]
    sine_part = jnp.sin(angles)[:, None, :]
    shaped = projected.reshape(row_count, head_count, head_size)
    leading = shaped[:, :, :half_dim]
    trailing = shaped[:, :, half_dim:]
    turned = jnp.concatenate(
        [leading * cosine - trailing * sine_part, trailing * cosine + leading * sine_part], axis=2
    )
    return turned.reshape(row_count, columns).astype(jnp.bfloat16)


def attend(query_rows, key_rows):
    row_count = query_rows.shape[0]
    key_heads = key_rows.shape[1] // HEAD_DIM
    group_size = query_rows.shape[1] // key_rows.shape[1]
    sequences = row_count // SEQ
    grouped_query = query_rows.reshape(sequences, SEQ, key_heads, group_size, HEAD_DIM)
    grouped_key = key_rows.reshape(sequences, SEQ, key_heads, HEAD_DIM)
    scores = jnp.einsum(
        "bqkgd,bskd->bkgqs", grouped_query, grouped_key, preferred_element_type=jnp.float32
    ) * HEAD_DIM ** (-0.5)
    causal_mask = lax.broadcasted_iota(jnp.int32, (SEQ, SEQ), 0) >= lax.broadcasted_iota(
        jnp.int32, (SEQ, SEQ), 1
    )
    scores = jnp.where(causal_mask, scores, -1e30)
    highest = jnp.max(scores, axis=4, keepdims=True)
    raised = jnp.exp(scores - highest)
    return (raised / jnp.sum(raised, axis=4, keepdims=True)).astype(jnp.bfloat16)


def mix_values(attention, value_rows):
    sequences = attention.shape[0]
    key_heads = attention.shape[1]
    group_size = attention.shape[2]
    grouped_value = value_rows.reshape(sequences, SEQ, key_heads, HEAD_DIM)
    combined = jnp.einsum(
        "bkgqs,bskd->bqkgd", attention, grouped_value, preferred_element_type=jnp.float32
    )
    return combined.reshape(sequences * SEQ, key_heads * group_size * HEAD_DIM)


def spread_back(attention, upstream):
    sequences = attention.shape[0]
    key_heads = attention.shape[1]
    group_size = attention.shape[2]
    grouped_upstream = upstream.reshape(sequences, SEQ, key_heads, group_size, HEAD_DIM)
    spread = jnp.einsum(
        "bkgqs,bqkgd->bskd", attention, grouped_upstream, preferred_element_type=jnp.float32
    )
    return spread.reshape(sequences * SEQ, key_heads * HEAD_DIM)


def body(hidden, norm_gain, query_weight, key_weight, value_weight, output_weight, probe_seed):
    seed_value = probe_seed[0]
    normed = normalize(hidden, norm_gain)
    model_width = normed.shape[1]
    query_width = query_weight.shape[1]
    key_width = key_weight.shape[1]
    head_count = query_width // HEAD_DIM
    key_heads = key_width // HEAD_DIM
    contract_rows = (((0,), (0,)), ((), ()))
    contract_columns = (((1,), (1,)), ((), ()))
    portions = in_one_piece((query_weight, key_weight, value_weight), "fsdp", 0, 1)
    query_raw = jnp.dot(normed, portions[0], preferred_element_type=jnp.float32)
    key_raw = jnp.dot(normed, portions[1], preferred_element_type=jnp.float32)
    value_raw = jnp.dot(normed, portions[2], preferred_element_type=jnp.float32)
    query_rows = rotate(query_raw, head_count)
    key_rows = rotate(key_raw, key_heads)
    value_rows = value_raw.astype(jnp.bfloat16)
    attention = attend(query_rows, key_rows)
    context = mix_values(attention, value_rows).astype(jnp.bfloat16)
    signs_value = sign_table(seed_value, 0, model_width, key_width)
    signs_out = sign_table(seed_value, 1, query_width, model_width)
    tangent_value = (
        jnp.dot(normed, signs_value, preferred_element_type=jnp.float32) * model_width ** (-0.5)
    ).astype(jnp.bfloat16)
    tangent_context = mix_values(attention, tangent_value).astype(jnp.bfloat16)
    probe_part = jnp.dot(context, signs_out, preferred_element_type=jnp.float32) * query_width ** (
        -0.5
    )
    whole_out = lax.all_gather(output_weight, "fsdp", axis=0, tiled=True)
    forward_part = jnp.dot(tangent_context, whole_out, preferred_element_type=jnp.float32)
    cotangent = (forward_part + probe_part).astype(jnp.bfloat16)
    back_context = lax.dot_general(
        cotangent, whole_out, contract_columns, preferred_element_type=jnp.float32
    )
    back_value = spread_back(attention, back_context.astype(jnp.bfloat16)).astype(jnp.bfloat16)
    portion = normed
    value_share = sent_and_summed(
        lax.dot_general(
            portion, back_value, contract_rows, preferred_element_type=jnp.float32
        ).astype(jnp.bfloat16),
        "fsdp",
        0,
    )
    portion = context
    output_share = lax.psum_scatter(
        lax.dot_general(
            portion, cotangent, contract_rows, preferred_element_type=jnp.float32
        ).astype(jnp.bfloat16),
        "fsdp",
        scatter_dimension=0,
        tiled=True,
    )
    curvature_value, curvature_output = (
        sent_and_summed(value_share.astype(jnp.bfloat16), "probe", 1),
        sent_and_summed(output_share, "probe", 1),
    )
    return (curvature_value, curvature_output)


def solution(mesh):
    return jax.shard_map(
        body,
        mesh=mesh,
        in_specs=(
            P(("probe", "fsdp"), None),
            P(),
            P("fsdp", None),
            P("fsdp", None),
            P("fsdp", None),
            P("fsdp", None),
            P("probe"),
        ),
        out_specs=(P("fsdp", "probe"), P("fsdp", "probe")),
        check_vma=False,
    )
```

profile of v0, /device:TPU:0, one launch (start us, length us, event | category | flops | bytes accessed | tf_op | source)
XLA Modules:
  0.0 589.5 jit_solution(6584148597963998947)
XLA Ops:
  7.2 0.0 all-gather.3.cloned.1.call-start
  7.2 1.8 pad_maximum_fusion.2
  9.0 0.0 all-gather.3.cloned.1.call-update
  9.0 0.0 all-gather.5.cloned.1.call-start
  9.1 0.7 all-gather.5.cloned.1.call-update
  9.8 0.0 reduce-scatter.2.cloned.1.call-start
  10.5 0.7 convert_element_type.128
  11.2 2.1 fusion.20
  13.3 0.0 copy-start.2
  13.3 4.9 fusion.63
  18.1 1.0 reshape.128
  19.2 1.0 multiply_cosine_fusion
  20.1 166.4 %all-gather.3.cloned.1.call-done = bf16[2048,3072]{1,0:T(8,128)(2,1)} async-done(((bf16[64,3072]{1,0:T(8,128)(2,1)}), bf16[2048,3072]{1,0:T(8,128)(2,1)}) %all-gather.3.cloned.1.call-update) | async-done | bytes 12582928 | tf_op jit(solution)/shard_map/all_gather | solution.py:16
  186.6 0.0 copy-done.2
  186.6 2.9 fusion.57
  189.5 1.0 reshape.131
  190.4 7.2 %fusion.30 = f32[64,8,16,128]{3,1,2,0:T(8,128)S(1)} fusion(bf16[2048,3072]{1,0:T(8,128)(2,1)} %all-gather.3.cloned.1.call-done, bf16[512,2048]{1,0:T(8,128)(2,1)S(1)} %copy-done.2, f32[2048]{0:T(1024)S(1)} %convert_element_type.128, f32[512]{0:T(512)S(1)} %add_rsqrt_fusion), kind=kOutput, calls=%fused_computation.49 | convolution fusion | flops 4299161600 | bytes 14690304 | tf_op jit(solution)/shard_map/dot_general | solution.py:129
  197.6 2.9 copy.83
  200.5 3.0 fusion.36
  203.5 0.1 fusion.102
  203.6 0.3 copy.79
  203.9 0.3 copy.78
  204.2 0.0 copy-start.1
  204.2 0.3 subtract_convert_fusion.1
  204.5 0.3 pad_maximum_fusion.1
  204.8 1.6 copy-done.1
  206.5 1.3 fusion.101
  207.8 2.8 subtract_convert_fusion
  210.6 1.2 pad_maximum_fusion
  211.8 1.3 fusion.40
  213.0 2.6 fusion.103
  215.6 0.0 copy-start.5
  215.6 1.1 divide_convert_fusion
  216.7 0.0 copy-start
  216.7 2.0 copy-done
  218.7 0.8 convert_bitcast_fusion
  219.5 3.1 copy.59
  222.6 4.5 convert_element_type.143
  227.1 3.0 convert_bitcast_fusion.1
  230.1 3.1 copy.56
  233.2 4.5 convert_element_type.139
  237.7 115.3 %all-gather.5.cloned.1.call-done = bf16[2048,2048]{1,0:T(8,128)(2,1)} async-done(((bf16[64,2048]{1,0:T(8,128)(2,1)}), bf16[2048,2048]{1,0:T(8,128)(2,1)}) %all-gather.5.cloned.1.call-update) | async-done | bytes 8388624 | tf_op jit(solution)/shard_map/all_gather | solution.py:146
  353.0 8.0 %fusion.104 = f32[512,2048]{1,0:T(8,128)S(1)} fusion(bf16[512,2048]{1,0:T(8,128)(2,1)} %convert_element_type.139, bf16[2048,2048]{1,0:T(8,128)(2,1)} %all-gather.5.cloned.1.call-done), kind=kOutput, calls=%fused_computation.127 | convolution fusion | flops 4294967296 | bytes 14680064 | tf_op jit(solution)/shard_map/dot_general | solution.py:147
  361.0 10.0 %add_convert_fusion = bf16[512,2048]{1,0:T(8,128)(2,1)S(1)} fusion(f32[512,2048]{1,0:T(8,128)S(1)} %fusion.104, bf16[512,2048]{1,0:T(8,128)(2,1)S(1)} %copy-done.3, s32[]{:T(128)S(6)} %add.79, s32[2048]{0:T(1024)S(1)} %iota_multiply_fusion), kind=kOutput, calls=%fused_computation.40 | convolution fusion | flops 4361027584 | bytes 8396804 | tf_op jit(solution)/shard_map/dot_general | solution.py:143
  371.0 1.3 copy-done.6
  372.3 6.8 %convolution_convert_fusion = bf16[2048,2048]{1,0:T(8,128)(2,1)} fusion(bf16[512,2048]{1,0:T(8,128)(2,1)S(1)} %copy-done.3, bf16[512,2048]{1,0:T(8,128)(2,1)S(1)} %add_convert_fusion), kind=kOutput, calls=%fused_computation.26 | convolution fusion | flops 4299161600 | bytes 12582912 | tf_op jit(solution)/shard_map/dot_general | solution.py:163
  379.1 0.0 reduce-scatter.2.cloned.1.call-update
  379.1 1.6 copy-done.7
  380.7 9.3 %convolution_convert_fusion.2 = bf16[512,2048]{1,0:T(8,128)(2,1)} fusion(bf16[512,2048]{1,0:T(8,128)(2,1)S(1)} %copy-done.7, bf16[2048,2048]{1,0:T(8,128)(2,1)} %all-gather.5.cloned.1.call-done), kind=kOutput, calls=%fused_computation.48 | convolution fusion | flops 4296015872 | bytes 12582912 | tf_op jit(solution)/shard_map/dot_general | solution.py:149
  390.0 3.2 reshape.132
  393.2 3.7 fusion.64
  396.9 0.3 copy.62
  397.2 3.0 convolution_convert_fusion.1
  400.2 42.1 %all_to_all.15 = bf16[32,64,512]{2,1,0:T(8,128)(2,1)S(1)} all-to-all(bf16[32,64,512]{2,1,0:T(8,128)(2,1)S(1)} %bitcast.61), channel_id=1, replica_groups=mesh['probe'=4,'fsdp'=32] {'fsdp'}, dimensions={0} | all-to-all | bytes 4194304 | tf_op jit(solution)/shard_map/all_to_all | solution.py:31
  442.3 0.3 reduce_sum.50
  442.6 0.6 copy.63
  443.3 3.3 all-to-all-start.1
  446.6 122.6 %reduce-scatter.2.cloned.1.call-done = bf16[64,2048]{1,0:T(8,128)(2,1)} async-done(((bf16[2048,2048]{1,0:T(8,128)(2,1)}), bf16[64,2048]{1,0:T(8,128)(2,1)}) %reduce-scatter.2.cloned.1.call-update) | async-done | bytes 262160 | tf_op jit(solution)/shard_map/reduce_scatter | solution.py:162
  569.1 1.7 copy.110
  570.8 0.0 all-to-all-done.1
  570.8 3.8 all-to-all-start.2
  574.6 0.6 convert_reduce_fusion.1
  575.2 6.9 %all-to-all-done.2 = bf16[4,64,512]{2,1,0:T(8,128)(2,1)S(1)} async-done(((bf16[4,64,512]{2,1,0:T(8,128)(2,1)}), bf16[4,64,512]{2,1,0:T(8,128)(2,1)S(1)}, u32[]{:S(2)}, u32[]{:S(2)}) %all-to-all-start.2) | async-done | bytes 262176 | tf_op jit(solution)/shard_map/all_to_all | solution.py:31
  582.1 0.7 convert_reduce_fusion
  (14 shorter events, 0.1 us)
Async XLA Ops:
  7.2 179.4 %all-gather.3.cloned.1.call-start = ((), (), s32[]{:S(2)}) async-start(), calls=%async_computation.4 | async-start | bytes 12976128 | tf_op jit(solution)/shard_map/all_gather | solution.py:16
  9.0 344.0 %all-gather.5.cloned.1.call-start = ((), (), s32[]{:S(2)}) async-start(), calls=%async_computation.5 | async-start | bytes 8650752 | tf_op jit(solution)/shard_map/all_gather | solution.py:146
  9.8 559.3 %reduce-scatter.2.cloned.1.call-start = ((), (), s32[]{:S(2)}) async-start(), calls=%async_computation.6 | async-start | bytes 8650752 | tf_op jit(solution)/shard_map/reduce_scatter | solution.py:162
  13.3 173.3 %copy-start.2 = (bf16[512,2048]{1,0:T(8,128)(2,1)S(1)}, bf16[512,2048]{1,0:T(8,128)(2,1)}, u32[]{:S(2)}) copy-start(bf16[512,2048]{1,0:T(8,128)(2,1)} %param.7) | copy-start | bytes 6291460
  204.2 2.2 copy-start.1
  215.6 3.1 copy-start.5
  216.7 2.0 copy-start
  219.5 7.6 %copy-start.4 = (bf16[2,256,4,128]{3,2,1,0:T(4,128)(2,1)S(1)}, bf16[2,256,4,128]{3,2,1,0:T(4,128)(2,1)}, u32[]{:S(2)}) copy-start(bf16[2,256,4,128]{3,2,1,0:T(4,128)(2,1)} %reshape.128) | copy-start | bytes 1572868
  237.7 123.3 %copy-start.3 = (bf16[512,2048]{1,0:T(8,128)(2,1)S(1)}, bf16[512,2048]{1,0:T(8,128)(2,1)}, u32[]{:S(2)}) copy-start(bf16[512,2048]{1,0:T(8,128)(2,1)} %convert_element_type.143) | copy-start | bytes 6291460
  371.0 1.3 copy-start.6
  379.1 1.6 copy-start.7
  443.3 127.5 %all-to-all-start.1 = ((bf16[4,64,128]{2,1,0:T(8,128)(2,1)}), bf16[4,64,128]{2,1,0:T(8,128)(2,1)S(1)}, u32[]{:S(2)}, u32[]{:S(2)}) async-start(bf16[4,64,128]{2,1,0:T(8,128)(2,1)} %copy.63), calls=%async_computation.1 | async-start | bytes 131072 | tf_op jit(solution)/shard_map/all_to_all | solution.py:31
  570.8 11.3 %all-to-all-start.2 = ((bf16[4,64,512]{2,1,0:T(8,128)(2,1)}), bf16[4,64,512]{2,1,0:T(8,128)(2,1)S(1)}, u32[]{:S(2)}, u32[]{:S(2)}) async-start(bf16[4,64,512]{2,1,0:T(8,128)(2,1)} %bitcast.58), calls=%async_computation.3 | async-start | bytes 524288 | tf_op jit(solution)/shard_map/all_to_all | solution.py:31
Sparse Core Ops, SparseCore 0:
  9.6 176.9 all-gather.2
  188.2 164.7 all-gather.4
  379.2 189.8 reduce-scatter.1
where the time goes:
time: 596 us; the launch traced here: 589 us
  waiting for transfers between devices  412 us (69%)
  matrix products  63.7 us (11%)
  blocking collectives  42.1 us (7%)
  local copies, waits for them, and re-layouts  34.3 us (6%)
  other arithmetic  15.4 us (3%)
  between operations  14.8 us (2%)
  starting transfers between devices  7.17 us (1%)
    all_gather x1, waiting for transfers between devices, in_one_piece(): lax.all_gather(both, axis, axis=dim, tiled=True)  166 us
    reduce_scatter x1, waiting for transfers between devices, body(): lax.psum_scatter(lax.dot_general(portion, cotangent, contract_rows, prefe...  123 us
    all_gather x1, waiting for transfers between devices, body(): whole_out = lax.all_gather(output_weight, 'fsdp', axis=0, tiled=True)  115 us
    all_to_all x1, blocking collectives, sent_and_summed(): parts = lax.all_to_all(split_up(value, dim, size), axis, 0, 0, tiled=True)  42.1 us
  transfers between devices with their start and end apart: 5, of which 4 were waited for; matrix products, arithmetic and copies ran while one was open for 14% of the time, Pallas kernels for 0%

commit v1 on v0

--- a/solution.py
+++ b/solution.py
@@ -1,35 +1,371 @@
+import functools
+
 import jax
 import jax.numpy as jnp
 from jax import lax
+from jax.experimental import pallas as pl
+from jax.experimental.pallas import tpu as pltpu
 from jax.sharding import PartitionSpec as P
 
+MESH = pl.DeviceIdType.MESH
 HEAD_DIM = 128
 SEQ = 256
-
-
 norm_eps = 1e-05
 rope_base = 500000.0
-
-
-def in_one_piece(arrays, axis, dim, along):
-    both = jnp.concatenate(arrays, axis=along)
-    result, at, finished = (lax.all_gather(both, axis, axis=dim, tiled=True), 0, [])
-    for a in arrays:
-        finished.append(lax.slice_in_dim(result, at, at + a.shape[along], axis=along))
-        at += a.shape[along]
-    return tuple(finished)
-
-
-def split_up(value, dim, size):
-    dims = value.shape
-    parts = value.reshape(*dims[:dim], size, dims[dim] // size, *dims[dim + 1 :])
-    return jnp.moveaxis(parts, dim, 0)
-
-
-def sent_and_summed(value, axis, dim):
-    size = lax.axis_size(axis)
-    parts = lax.all_to_all(split_up(value, dim, size), axis, 0, 0, tiled=True)
-    return jnp.sum(parts.astype(jnp.float32), axis=0)
+ORDERS = (("z", "x", "y"), ("x", "y", "z"), ("z", "y", "x"), ("y", "x", "z"))
+
+
+class Place:
+    def __init__(self):
+        p = lax.axis_index("probe")
+        f = lax.axis_index("fsdp")
+        self.p, self.f = p, f
+        self.x = lax.rem(f, 4)
+        self.zl = lax.rem(lax.div(f, 4), 2)
+        self.y = lax.div(f, 8)
+        self.zh = lax.div(p, 2)
+        self.c = lax.rem(p, 2)
+        self.z = self.zh * 2 + self.zl
+
+    def move(self, axis, step):
+        x, y, z = self.x, self.y, self.z
+        if axis == "x":
+            x = lax.rem(x + step + 4, 4)
+        elif axis == "y":
+            y = lax.rem(y + step + 4, 4)
+        else:
+            z = lax.rem(z + step + 4, 4)
+        return (lax.div(z, 2) * 2 + self.c, y * 8 + lax.rem(z, 2) * 4 + x)
+
+    def partner(self):
+        return (self.zh * 2 + 1 - self.c, self.f)
+
+    def neighbours(self):
+        return [self.move(a, s) for a in ("x", "y", "z") for s in (1, -1)] + [self.partner()]
+
+
+def meet(place):
+    barrier = pltpu.get_barrier_semaphore()
+    peers = place.neighbours()
+    for peer in peers:
+        pl.semaphore_signal(barrier, inc=1, device_id=peer, device_id_type=MESH)
+    pl.semaphore_wait(barrier, len(peers))
+
+
+class Copies:
+    def __init__(self, send_sems, recv_sems):
+        self.send_sems, self.recv_sems = send_sems, recv_sems
+        self.used = 0
+        self.started = []
+
+    def slot(self):
+        self.used += 1
+        return self.used - 1
+
+    def send(self, slot, ref, peer, dst=None):
+        copy = pltpu.make_async_remote_copy(
+            src_ref=ref,
+            dst_ref=ref if dst is None else dst,
+            send_sem=self.send_sems.at[slot],
+            recv_sem=self.recv_sems.at[slot],
+            device_id=peer,
+            device_id_type=MESH,
+        )
+        copy.start()
+        self.started.append(copy)
+
+    def wait_recv(self, slot, ref, peer):
+        pltpu.make_async_remote_copy(
+            src_ref=ref,
+            dst_ref=ref,
+            send_sem=self.send_sems.at[slot],
+            recv_sem=self.recv_sems.at[slot],
+            device_id=peer,
+            device_id_type=MESH,
+        ).wait_recv()
+
+    def finish(self):
+        for copy in self.started:
+            copy.wait_send()
+
+
+def gather_steps(buf, order, place, copies):
+    both = slice(None)
+
+    def region(have, where, core, halves):
+        def pick(axis, extent):
+            return pl.ds(0, extent) if axis in have else pl.ds(where[axis], 1)
+
+        return buf.at[pick("y", 4), pick("z", 2), pick("x", 4), core, halves]
+
+    here = {"x": place.x, "y": place.y, "z": place.zl}
+    core, other = place.c, 1 - place.c
+    partner = place.partner()
+    from_partner = []
+
+    def share(have, where):
+        slot = copies.slot()
+        copies.send(slot, region(have, where, core, pl.ds(0, 2)), partner)
+        from_partner.append((slot, region(have, where, other, pl.ds(0, 2))))
+
+    have = ()
+    for phase, axis in enumerate(order):
+        last = phase == 2
+        if last:
+            share(have, here)
+        if axis == "z":
+            slots = (copies.slot(), copies.slot())
+            for half, step in ((0, 1), (1, -1)):
+                copies.send(
+                    slots[half], region(have, here, core, pl.ds(half, 1)), place.move("z", step)
+                )
+            yield
+            there = dict(here, z=1 - place.zl)
+            for half, step in ((0, -1), (1, 1)):
+                copies.wait_recv(
+                    slots[half], region(have, there, core, pl.ds(half, 1)), place.move("z", step)
+                )
+            if last:
+                share(have, there)
+        else:
+            at = {s: dict(here, **{axis: lax.rem(here[axis] + s + 4, 4)}) for s in (-1, 1, 2)}
+            up, down, up2, down2 = (copies.slot() for _ in range(4))
+            ahead, behind = place.move(axis, 1), place.move(axis, -1)
+            copies.send(up, region(have, here, core, pl.ds(0, 2)), ahead)
+            copies.send(down, region(have, here, core, pl.ds(0, 2)), behind)
+            yield
+            copies.wait_recv(up, region(have, at[-1], core, pl.ds(0, 2)), behind)
+            copies.send(up2, region(have, at[-1], core, pl.ds(0, 1)), ahead)
+            copies.wait_recv(down, region(have, at[1], core, pl.ds(0, 2)), ahead)
+            copies.send(down2, region(have, at[1], core, pl.ds(1, 1)), behind)
+            if last:
+                share(have, at[-1])
+                share(have, at[1])
+            yield
+            copies.wait_recv(up2, region(have, at[2], core, pl.ds(0, 1)), behind)
+            copies.wait_recv(down2, region(have, at[2], core, pl.ds(1, 1)), ahead)
+            if last:
+                share(have, at[2])
+        have = have + (axis,)
+    yield
+    for slot, ref in from_partner:
+        copies.wait_recv(slot, ref, partner)
+
+
+def in_turn(walks):
+    walks = list(walks)
+    while walks:
+        left = []
+        for walk in walks:
+            try:
+                next(walk)
+                left.append(walk)
+            except StopIteration:
+                pass
+        walks = left
+
+
+def gather_kernel(wq, wk, wv, wo, qkv_out, out_out, qkv, out, send_sems, recv_sems, load_sems, store_sems):
+    place = Place()
+    loads = []
+
+    def load(src, dst):
+        copy = pltpu.make_async_copy(src, dst, load_sems.at[len(loads)])
+        copy.start()
+        loads.append(copy)
+
+    def own(buf, columns):
+        return buf.at[place.y, place.zl, place.x, place.c, :, :, columns]
+
+    def rows(w, columns):
+        return w.at[place.c, :, :, columns]
+
+    for h in range(4):
+        load(rows(wq, pl.ds(h * 512, 512)), own(qkv.at[h], pl.ds(0, 512)))
+        load(rows(wk, pl.ds(h * 128, 128)), own(qkv.at[h], pl.ds(512, 128)))
+        load(rows(wv, pl.ds(h * 128, 128)), own(qkv.at[h], pl.ds(640, 128)))
+    for j in range(4):
+        load(rows(wo, pl.ds(j * 512, 512)), own(out.at[j], pl.ds(0, 512)))
+    meet(place)
+    for copy in loads:
+        copy.wait()
+    copies = Copies(send_sems, recv_sems)
+    in_turn([gather_steps(qkv.at[h], ORDERS[h], place, copies) for h in range(4)]+[gather_steps(out.at[h], ORDERS[h], place, copies) for h in range(4)])
+    stores = [
+        pltpu.make_async_copy(qkv, qkv_out, store_sems.at[0]),
+        pltpu.make_async_copy(out, out_out, store_sems.at[1]),
+    ]
+    for copy in stores:
+        copy.start()
+    copies.finish()
+    for copy in stores:
+        copy.wait()
+
+
+def gather_all(wq, wk, wv, wo):
+    halves = [w.reshape(2, 2, 16, w.shape[1]) for w in (wq, wk, wv, wo)]
+    shapes = [(4, 4, 2, 4, 2, 2, 16, 768), (4, 4, 2, 4, 2, 2, 16, 512)]
+    copies = 120
+    qkv, out = pl.pallas_call(
+        gather_kernel,
+        out_shape=[jax.ShapeDtypeStruct(s, jnp.bfloat16) for s in shapes],
+        in_specs=[pl.BlockSpec(memory_space=pl.ANY)] * 4,
+        out_specs=[pl.BlockSpec(memory_space=pl.ANY)] * 2,
+        scratch_shapes=[pltpu.VMEM(s, jnp.bfloat16) for s in shapes]
+        + [
+            pltpu.SemaphoreType.DMA((copies,)),
+            pltpu.SemaphoreType.DMA((copies,)),
+            pltpu.SemaphoreType.DMA((16,)),
+            pltpu.SemaphoreType.DMA((2,)),
+        ],
+        compiler_params=pltpu.CompilerParams(
+            collective_id=0, has_side_effects=True, vmem_limit_bytes=48 * 1024 * 1024
+        ),
+    )(*halves)
+    return qkv.reshape(4, 2048, 768), out.reshape(4, 2048, 512)
+
+
+REDUCE_ORDERS = (("x", "y", "z"), ("y", "z", "x"), ("x", "z", "y"), ("y", "x", "z"), ("z", "x", "y"))
+
+
+def wide(value):
+    return value.astype(jnp.float32)
+
+
+def reduce_steps(unit, order, mine, theirs, landing, result, place, copies, partner_slot):
+    here = {"x": place.x, "y": place.y, "z": place.z}
+
+    def region(done, where, half):
+        at = dict(where)
+
+        def pick(axis, extent):
+            return pl.ds(at[axis], 1) if axis in done else pl.ds(0, extent)
+
+        if "z" in done:
+            zh, zl = pl.ds(lax.div(at["z"], 2), 1), pl.ds(lax.rem(at["z"], 2), 1)
+        else:
+            zh, zl = pl.ds(0, 2), pl.ds(0, 2)
+        return mine.at[zh, pick("y", 4), zl, pick("x", 4), half]
+
+    copies.wait_recv(partner_slot, theirs, place.partner())
+
+    def add_partner(i, carry):
+        zh, y = lax.div(i, 4), lax.rem(i, 4)
+        mine[zh, y] = (wide(mine[zh, y]) + wide(theirs[zh, y])).astype(jnp.bfloat16)
+        return carry
+
+    lax.fori_loop(0, 8, add_partner, 0)
+    done = ()
+    for stage, axis in enumerate(order):
+        land = landing[stage]
+        done = done + (axis,)
+        at = {s: dict(here, **{axis: lax.rem(here[axis] + s + 4, 4)}) for s in (-1, 0, 1, 2)}
+        ahead, behind = place.move(axis, 1), place.move(axis, -1)
+        slots = [copies.slot() for _ in range(6)]
+
+        def send(slot, step, half, peer):
+            copies.send(slots[slot], region(done, at[step], half), peer, dst=land.at[slot])
+
+        def wait(slot, peer):
+            copies.wait_recv(slots[slot], land.at[slot], peer)
+
+        send(0, 2, 0, ahead)
+        send(1, 2, 1, behind)
+        send(3, 1, 1, ahead)
+        send(4, -1, 0, behind)
+        yield
+        for slot, step, half, source, peer, onward in (
+            (0, 1, 0, behind, ahead, 2),
+            (1, -1, 1, ahead, behind, 5),
+        ):
+            wait(slot, source)
+            part = region(done, at[step], half)
+            part[...] = (wide(part[...]) + wide(land[slot])).astype(jnp.bfloat16)
+            send(onward, step, half, peer)
+        yield
+        for slot, source in ((3, behind), (4, ahead), (2, behind), (5, ahead)):
+            wait(slot, source)
+        for half in (0, 1):
+            part = region(done, at[0], half)
+            total = wide(part[...]) + wide(land[2 + half]) + wide(land[4 + half])
+            if stage == 2:
+                result[pl.ds(32 * half, 32), :] = total.reshape(32, 128)
+            else:
+                part[...] = total.astype(jnp.bfloat16)
+
+
+def stage_shape(order, stage):
+    done = order[: stage + 1]
+    z = 1 if "z" in done else 2
+    return (6, z, 1 if "y" in done else 4, z, 1 if "x" in done else 4, 32, 128)
+
+
+def reduce_kernel(term_value, term_out, value_ref, out_ref, mine, theirs, *rest):
+    landing, (send_sems, recv_sems, load_sems) = rest[:15], rest[15:]
+    place = Place()
+    copies = Copies(send_sems, recv_sems)
+
+    def columns(unit, core):
+        ref = term_value if unit == 4 else term_out
+        start = 0 if unit == 4 else unit * 128
+        return ref.at[:, core, :, :, :, :, :, pl.ds(start, 128)]
+
+    loads = []
+    for unit in range(5):
+        copy = pltpu.make_async_copy(columns(unit, place.c), mine.at[unit], load_sems.at[unit])
+        copy.start()
+        loads.append(copy)
+    meet(place)
+    slots = []
+    for unit in range(5):
+        slots.append(copies.slot())
+        copies.send(slots[-1], columns(unit, 1 - place.c), place.partner(), dst=theirs.at[unit])
+    for copy in loads:
+        copy.wait()
+    in_turn(
+        reduce_steps(
+            unit,
+            REDUCE_ORDERS[unit],
+            mine.at[unit],
+            theirs.at[unit],
+            landing[3 * unit : 3 * unit + 3],
+            value_ref if unit == 4 else out_ref.at[:, pl.ds(128 * unit, 128)],
+            place,
+            copies,
+            slots[unit],
+        )
+        for unit in range(5)
+    )
+    copies.finish()
+
+
+def reduce_all(term_value, term_out):
+    table = (2, 4, 2, 4, 2, 32, 128)
+    operands = [t.reshape(2, 2, 4, 2, 4, 2, 32, t.shape[2]) for t in (term_value, term_out)]
+    copies = 5 + 5 * 18
+    return pl.pallas_call(
+        reduce_kernel,
+        out_shape=[
+            jax.ShapeDtypeStruct((64, 128), jnp.float32),
+            jax.ShapeDtypeStruct((64, 512), jnp.float32),
+        ],
+        in_specs=[pl.BlockSpec(memory_space=pl.ANY)] * 2,
+        out_specs=[pl.BlockSpec(memory_space=pltpu.VMEM)] * 2,
+        scratch_shapes=[pltpu.VMEM((5,) + table, jnp.bfloat16)] * 2
+        + [
+            pltpu.VMEM(stage_shape(REDUCE_ORDERS[unit], stage), jnp.bfloat16)
+            for unit in range(5)
+            for stage in range(3)
+        ]
+        + [
+            pltpu.SemaphoreType.DMA((copies,)),
+            pltpu.SemaphoreType.DMA((copies,)),
+            pltpu.SemaphoreType.DMA((5,)),
+        ],
+        compiler_params=pltpu.CompilerParams(
+            collective_id=1, has_side_effects=True, vmem_limit_bytes=48 * 1024 * 1024
+        ),
+    )(*operands)
 
 
 def sign_table(seed_value, matrix_code, row_total, column_total):
@@ -121,57 +457,48 @@
     model_width = normed.shape[1]
     query_width = query_weight.shape[1]
     key_width = key_weight.shape[1]
-    head_count = query_width // HEAD_DIM
-    key_heads = key_width // HEAD_DIM
     contract_rows = (((0,), (0,)), ((), ()))
-    contract_columns = (((1,), (1,)), ((), ()))
-    portions = in_one_piece((query_weight, key_weight, value_weight), "fsdp", 0, 1)
-    query_raw = jnp.dot(normed, portions[0], preferred_element_type=jnp.float32)
-    key_raw = jnp.dot(normed, portions[1], preferred_element_type=jnp.float32)
-    value_raw = jnp.dot(normed, portions[2], preferred_element_type=jnp.float32)
-    query_rows = rotate(query_raw, head_count)
-    key_rows = rotate(key_raw, key_heads)
+    wide_tables, out_tables = gather_all(query_weight, key_weight, value_weight, output_weight)
+    f32 = dict(preferred_element_type=jnp.float32)
+    query_raw = jnp.concatenate([jnp.dot(normed, wide_tables[h, :, :512], **f32) for h in range(4)], 1)
+    key_raw = jnp.concatenate([jnp.dot(normed, wide_tables[h, :, 512:640], **f32) for h in range(4)], 1)
+    value_raw = jnp.concatenate([jnp.dot(normed, wide_tables[h, :, 640:], **f32) for h in range(4)], 1)
+    query_rows = rotate(query_raw, query_width // HEAD_DIM)
+    key_rows = rotate(key_raw, key_width // HEAD_DIM)
     value_rows = value_raw.astype(jnp.bfloat16)
     attention = attend(query_rows, key_rows)
     context = mix_values(attention, value_rows).astype(jnp.bfloat16)
     signs_value = sign_table(seed_value, 0, model_width, key_width)
     signs_out = sign_table(seed_value, 1, query_width, model_width)
-    tangent_value = (
-        jnp.dot(normed, signs_value, preferred_element_type=jnp.float32) * model_width ** (-0.5)
-    ).astype(jnp.bfloat16)
+    tangent_value = (jnp.dot(normed, signs_value, **f32) * model_width ** (-0.5)).astype(jnp.bfloat16)
     tangent_context = mix_values(attention, tangent_value).astype(jnp.bfloat16)
-    probe_part = jnp.dot(context, signs_out, preferred_element_type=jnp.float32) * query_width ** (
-        -0.5
-    )
-    whole_out = lax.all_gather(output_weight, "fsdp", axis=0, tiled=True)
-    forward_part = jnp.dot(tangent_context, whole_out, preferred_element_type=jnp.float32)
+    probe_part = jnp.dot(context, signs_out, **f32) * query_width ** (-0.5)
+    forward_part = jnp.concatenate([jnp.dot(tangent_context, out_tables[j], **f32) for j in range(4)], 1)
     cotangent = (forward_part + probe_part).astype(jnp.bfloat16)
-    back_context = lax.dot_general(
-        cotangent, whole_out, contract_columns, preferred_element_type=jnp.float32
+    back_context = sum(
+        lax.dot_general(
+            cotangent[:, 512 * j : 512 * j + 512], out_tables[j], (((1,), (1,)), ((), ())), **f32
+        )
+        for j in range(4)
     )
     back_value = spread_back(attention, back_context.astype(jnp.bfloat16)).astype(jnp.bfloat16)
-    portion = normed
-    value_share = sent_and_summed(
-        lax.dot_general(
-            portion, back_value, contract_rows, preferred_element_type=jnp.float32
-        ).astype(jnp.bfloat16),
-        "fsdp",
-        0,
-    )
-    portion = context
-    output_share = lax.psum_scatter(
-        lax.dot_general(
-            portion, cotangent, contract_rows, preferred_element_type=jnp.float32
-        ).astype(jnp.bfloat16),
-        "fsdp",
-        scatter_dimension=0,
-        tiled=True,
-    )
-    curvature_value, curvature_output = (
-        sent_and_summed(value_share.astype(jnp.bfloat16), "probe", 1),
-        sent_and_summed(output_share, "probe", 1),
-    )
-    return (curvature_value, curvature_output)
+    term_value = jnp.stack(
+        [
+            lax.dot_general(normed, back_value[:, 128 * p : 128 * p + 128], contract_rows, **f32).astype(
+                jnp.bfloat16
+            )
+            for p in range(4)
+        ]
+    )
+    term_out = jnp.stack(
+        [
+            lax.dot_general(context, cotangent[:, 512 * p : 512 * p + 512], contract_rows, **f32).astype(
+                jnp.bfloat16
+            )
+            for p in range(4)
+        ]
+    )
+    return tuple(reduce_all(term_value, term_out))
 
 
 def solution(mesh):

time: 596 us -> 280 us (0.47)
  waiting for transfers between devices: 412 us -> 0 us
  Pallas kernels: 0 us -> 116 us
  blocking collectives: 42.1 us -> 0 us
  matrix products: 63.7 us -> 81.4 us
  local copies, waits for them, and re-layouts: 34.3 us -> 48.4 us
  between operations: 14.8 us -> 2.19 us
  other arithmetic: 15.4 us -> 27.6 us
  starting transfers between devices: 7.17 us -> 0 us
    all_gather x2 -> x0, waiting for transfers between devices: 282 us -> none  [the longest x1 166 us: in_one_piece(): lax.all_gather(both, axis, axis=dim, tiled=True)]
    reduce_scatter x1 -> x0, waiting for transfers between devices: 123 us -> none  [body(): lax.psum_scatter(lax.dot_general(portion, cotangent, contract_rows, prefe...]
    pallas_call x0 -> x2, Pallas kernels: none -> 116 us  [the longest x1 72.2 us: gather_all(): pl.pallas_call(gather_kernel, out_shape=[jax.ShapeDtypeStruct(s, jnp.bflo...]
    all_to_all x1 -> x0, blocking collectives: 42.1 us -> none  [sent_and_summed(): parts = lax.all_to_all(split_up(value, dim, size), axis, 0, 0, tiled=True)]
    dot_general x9 -> x30, matrix products: 54.9 us -> 66.2 us  [the longest x1 13.5 us: body(): probe_part = jnp.dot(context, signs_out, **f32) * query_width ** (-0.5)]
    another operation x2 -> x4, other arithmetic: 3.05 us -> 10.5 us
    all_to_all x2 -> x0, starting transfers between devices: 7.05 us -> none  [sent_and_summed(): parts = lax.all_to_all(split_up(value, dim, size), axis, 0, 0, tiled=True)]
    all_to_all x2 -> x0, waiting for transfers between devices: 6.89 us -> none  [sent_and_summed(): parts = lax.all_to_all(split_up(value, dim, size), axis, 0, 0, tiled=True)]
  transfers between devices with their start and end apart: 5 -> 0, of which waited for: 4 -> 0; matrix products, arithmetic and copies ran while one was open for 14% -> 0% of each run, Pallas kernels for 0% -> 0%
where the time goes in v1:
time: 280 us; the launch traced here: 275 us
  Pallas kernels  116 us (41%)
  matrix products  81.4 us (29%)
  local copies, waits for them, and re-layouts  48.4 us (17%)
  other arithmetic  27.6 us (10%)
    pallas_call x1, Pallas kernels, gather_all(): pl.pallas_call(gather_kernel, out_shape=[jax.ShapeDtypeStruct(s, jnp.bflo...  72.2 us
    pallas_call x1, Pallas kernels, reduce_all(): pl.pallas_call(reduce_kernel, out_shape=[jax.ShapeDtypeStruct((64, 128),...  43.5 us
    unnamed x31, local copies, waits for them, and re-layouts  14.7 us
    dot_general x1, matrix products, body(): probe_part = jnp.dot(context, signs_out, **f32) * query_width ** (-0.5)  13.5 us
    dot_general x4, matrix products, body(): jnp.dot(normed, wide_tables[h, :, :512], **f32)  11.5 us
    convert_element_type x2, local copies, waits for them, and re-layouts, body(): context = mix_values(attention, value_rows).astype(jnp.bfloat16)  9.06 us
    convert_element_type x2, local copies, waits for them, and re-layouts, body(): tangent_context = mix_values(attention, tangent_value).astype(jnp.bfloat16)  8.98 us
    sub x1, other arithmetic, attend(): raised = jnp.exp(scores - highest)  8.96 us

profile of v1, /device:TPU:0, one launch (start us, length us, event | category | flops | bytes accessed | tf_op | source)
XLA Modules:
  0.0 275.2 jit_solution(18394296800999093611)
XLA Ops:
  1.3 2.2 fusion.18
  3.6 1.8 multiply_cosine_fusion
  5.4 0.5 fusion.20
  6.0 3.3 %fusion.64 = bf16[512,512]{1,0:T(8,128)(2,1)} fusion(bf16[512,2048]{1,0:T(8,128)(2,1)S(1)} %fusion.20, s32[]{:T(128)} %bitcast, s32[2048]{0:T(1024)S(1)} %iota_multiply_fusion.1), kind=kOutput, calls=%fused_computation.95 | convolution fusion | flops 1089994752 | bytes 2629636 | tf_op jit(solution)/shard_map/dot_general | solution.py:473
  9.3 2.0 reshape.152
  11.3 72.2 %shard_map.86 = (bf16[4,4,2,4,2,2,16,768]{7,6,5,4,3,2,1,0:T(8,128)(2,1)}, bf16[4,4,2,4,2,2,16,512]{7,6,5,4,3,2,1,0:T(8,128)(2,1)}) custom-call(bf16[2,2,16,2048]{3,2,1,0:T(8,128)(2,1)S(1)} %bitcast.141, bf16[2,2,16,512]{3,2,1,0:T(8,128)(2,1)S(1)} %bitcast.143, bf16[2,2,16,512]{3,2,1,0:T(8,128)(2,1)S(1)} %bitcast.144, bf16[2,2,16,2048]{3,2,1,0:T(8,128)(2,1)S(1)} %bitcast.142), custom_call_target="tpu_custom_call" | custom-call | tf_op jit(solution)/shard_map/pallas_call | solution.py:209
  83.6 1.9 convolution_convert_fusion.8
  85.4 1.9 convolution_convert_fusion.9
  87.3 1.9 convolution_convert_fusion.10
  89.2 1.9 convolution_convert_fusion.11
  91.1 0.9 convert_element_type.155
  92.0 1.9 fusion.68
  93.9 1.9 fusion.69
  95.7 1.9 fusion.70
  97.6 1.9 fusion.71
  99.6 1.1 fusion.116
  100.6 1.4 copy.47
  102.0 2.4 copy.46
  104.4 1.5 subtract_convert_fusion.1
  105.9 0.3 pad_maximum_fusion.5
  106.2 2.9 %fusion.38 = f32[512,512]{0,1:T(8,128)S(1)} fusion(bf16[512,2048]{1,0:T(8,128)(2,1)S(1)} %fusion.20, bf16[4,2048,768]{2,1,0:T(8,128)(2,1)} %bitcast.173), kind=kOutput, calls=%fused_computation.66 | convolution fusion | flops 1073741824 | bytes 5242880 | tf_op jit(solution)/shard_map/dot_general | solution.py:463
  109.1 2.9 %fusion.39 = f32[512,512]{0,1:T(8,128)S(1)} fusion(bf16[512,2048]{1,0:T(8,128)(2,1)S(1)} %fusion.20, bf16[4,2048,768]{2,1,0:T(8,128)(2,1)} %bitcast.174), kind=kOutput, calls=%fused_computation.68 | convolution fusion | flops 1073741824 | bytes 5242880 | tf_op jit(solution)/shard_map/dot_general | solution.py:463
  112.0 2.9 %fusion.40 = f32[512,512]{0,1:T(8,128)S(1)} fusion(bf16[512,2048]{1,0:T(8,128)(2,1)S(1)} %fusion.20, bf16[4,2048,768]{2,1,0:T(8,128)(2,1)} %bitcast.175), kind=kOutput, calls=%fused_computation.70 | convolution fusion | flops 1073741824 | bytes 5242880 | tf_op jit(solution)/shard_map/dot_general | solution.py:463
  114.9 2.9 %fusion.41 = f32[512,512]{0,1:T(8,128)S(1)} fusion(bf16[512,2048]{1,0:T(8,128)(2,1)S(1)} %fusion.20, bf16[4,2048,768]{2,1,0:T(8,128)(2,1)} %bitcast.176), kind=kOutput, calls=%fused_computation.72 | convolution fusion | flops 1073741824 | bytes 5242880 | tf_op jit(solution)/shard_map/dot_general | solution.py:463
  117.8 0.9 pad_maximum_fusion.1
  118.7 2.7 fusion.115
  121.4 3.8 %copy.49 = f32[512,16,64]{2,0,1:T(8,128)} copy(f32[512,16,64]{0,2,1:T(8,128)} %get-tuple-element.12) | data formatting | bytes 4194304
  125.2 3.8 %copy.48 = f32[512,16,64]{2,0,1:T(8,128)} copy(f32[512,16,64]{0,2,1:T(8,128)} %get-tuple-element.13) | data formatting | bytes 4194304
  129.0 4.6 %subtract_convert_fusion = (bf16[512,16,64]{2,0,1:T(8,128)(2,1)S(1)}, bf16[512,16,64]{2,0,1:T(8,128)(2,1)S(1)}) fusion(f32[512,16,64]{2,0,1:T(8,128)} %copy.49, f32[512,16,64]{2,0,1:T(8,128)} %copy.48, f32[512,64]{1,0:T(8,128)S(1)} %copy-done.6, f32[512,64]{1,0:T(8,128)S(1)} %get-tuple-element.18), kind=kLoop, calls=%fused_computation.45 | loop fusion | flops 4194304 | bytes 6553600 | tf_op jit(solution)/shard_map/convert.4
  133.7 1.2 pad_maximum_fusion.2
  134.8 4.5 %fusion.44 = f32[2,4,256,256,4]{3,2,4,1,0:T(8,128)} fusion(bf16[2,256,4,4,128]{4,1,0,3,2:T(8,128)(2,1)S(1)} %bitcast.147, bf16[2,256,4,128,1]{3,1,0,2,4:T(8,128)(2,1)S(1)} %bitcast.164), kind=kOutput, calls=%fused_computation.77 | convolution fusion | flops 536870912 | bytes 11010048 | tf_op jit(solution)/shard_map/bqkgd,bskd->bkgqs/dot_general | solution.py:420
  139.3 9.0 %fusion.117 = (f32[2,4,4,256]{3,2,1,0:T(4,128)S(1)}, f32[2,4,4,256,256]{3,4,2,1,0:T(8,128)S(1)}) fusion(f32[2,4,256,256,4]{3,2,4,1,0:T(8,128)} %fusion.44, pred[256,256]{0,1:T(8,128)(4,1)S(1)} %iota_compare_fusion), kind=kOutput, calls=%fused_computation.173 | output fusion | flops 12583167 | bytes 16875520 | tf_op jit(solution)/shard_map/sub | solution.py:428
  148.3 1.1 divide_convert_fusion
  149.4 1.9 copy-done.4
  151.4 2.1 convert_bitcast_fusion
  153.4 4.5 %copy.27 = bf16[2,256,4,4,128]{4,3,2,1,0:T(4,128)(2,1)} copy(bf16[2,256,4,4,128]{1,4,3,2,0:T(8,128)(2,1)} %convert_bitcast_fusion) | data formatting | bytes 4194304 | tf_op jit(solution)/shard_map/convert_element_type | solution.py:470
  157.9 4.6 %convert_element_type.158 = bf16[512,2048]{1,0:T(8,128)(2,1)} reshape(bf16[2,256,4,4,128]{4,3,2,1,0:T(4,128)(2,1)} %copy.27) | data formatting | bytes 4194304 | tf_op jit(solution)/shard_map/convert_element_type | solution.py:470
  162.5 4.3 %convert_bitcast_fusion.1 = bf16[2,256,4,4,128]{1,4,3,2,0:T(8,128)(2,1)} fusion(bf16[2,4,4,256,256]{3,4,2,1,0:T(8,128)(2,1)} %copy-done.4, bf16[2,256,4,128,1]{3,2,1,0,4:T(4,128)(2,1)S(1)} %bitcast.162), kind=kOutput, calls=%fused_computation.80 | convolution fusion | flops 537919488 | bytes 6815744 | tf_op jit(solution)/shard_map/bkgqs,bskd->bqkgd/dot_general | solution.py:437
  166.8 4.5 %copy.24 = bf16[2,256,4,4,128]{4,3,2,1,0:T(4,128)(2,1)} copy(bf16[2,256,4,4,128]{1,4,3,2,0:T(8,128)(2,1)} %convert_bitcast_fusion.1) | data formatting | bytes 4194304 | tf_op jit(solution)/shard_map/convert_element_type | solution.py:474
  171.3 4.5 %convert_element_type.154 = bf16[512,2048]{1,0:T(8,128)(2,1)} reshape(bf16[2,256,4,4,128]{4,3,2,1,0:T(4,128)(2,1)} %copy.24) | data formatting | bytes 4194304 | tf_op jit(solution)/shard_map/convert_element_type | solution.py:474
  175.8 4.2 %fusion.114 = (bf16[1,4,2,4,2,2,16,512]{7,6,5,4,3,2,1,0:T(8,128)(2,1)S(1)}, bf16[1,4,2,4,2,2,16,512]{7,6,5,4,3,2,1,0:T(8,128)(2,1)S(1)}, bf16[1,4,2,4,2,2,16,512...) fusion(bf16[4,4,2,4,2,2,16,512]{7,6,5,4,3,2,1,0:T(8,128)(2,1)} %get-tuple-element.5), kind=kLoop, calls=%fused_computation.170 | loop fusion | bytes 16777216 | tf_op jit(solution)/shard_map/slice | solution.py:476
  180.0 1.3 fusion.121
  181.3 2.3 fusion.118
  183.5 2.3 fusion.120
  185.8 2.3 fusion.119
  188.1 13.5 %fusion.25 = bf16[512,2048]{0,1:T(8,128)(2,1)S(1)} fusion(f32[512,512]{0,1:T(8,128)S(1)} %fusion.121, f32[512,512]{0,1:T(8,128)} %fusion.120, f32[512,512]{0,1:T(8,128)} %fusion.119, f32[512,512]{0,1:T(8,128)} %fusion.118, bf16[512,2048]{1,0:T(8,128)(2,1)S(1)} %copy-done.7, s32[]{:T(128)S(6)} %add.86, s32[2048]{0:T(1024)S(1)} %iota_multiply_fusion), kind=kOutput, calls=%fused_computation.40 | convolution fusion | flops 4364173312 | bytes 8396804 | tf_op jit(solution)/shard_map/dot_general | solution.py:475
  201.6 1.3 fusion.29
  202.9 1.3 fusion.30
  204.3 1.3 fusion.31
  205.6 1.3 fusion.32
  206.9 4.1 %pad_maximum_fusion = bf16[4,2048,512]{2,1,0:T(8,128)(2,1)} fusion(bf16[1,2048,512]{2,1,0:T(8,128)(2,1)S(1)} %fusion.32, bf16[1,2048,512]{2,1,0:T(8,128)(2,1)S(1)} %fusion.31, bf16[1,2048,512]{2,1,0:T(8,128)(2,1)S(1)} %fusion.30, bf16[1,2048,512]{2,1,0:T(8,128)(2,1)S(1)} %fusion.29), kind=kLoop, calls=%fused_computation.10 | loop fusion | flops 12582912 | bytes 16777216 | tf_op jit(solution)/shard_map/stack | solution.py:493
  211.0 1.3 fusion.78
  212.3 1.3 fusion.81
  213.6 1.3 fusion.84
  214.9 2.7 add_convert_fusion
  217.6 4.4 %reshape.160 = bf16[2,256,4,4,128]{4,3,2,1,0:T(4,128)(2,1)} reshape(bf16[512,2048]{1,0:T(8,128)(2,1)} %add_convert_fusion) | data formatting | bytes 4194304 | tf_op jit(solution)/shard_map/reshape | solution.py:447
  222.0 4.3 %fusion.65 = bf16[2,256,4,128]{1,3,2,0:T(8,128)(2,1)S(1)} fusion(bf16[2,4,4,256,256]{3,4,2,1,0:T(8,128)(2,1)} %copy-done.4, bf16[2,256,4,4,128]{4,3,2,1,0:T(4,128)(2,1)} %reshape.160), kind=kOutput, calls=%fused_computation.96 | convolution fusion | flops 537133056 | bytes 6815744 | tf_op jit(solution)/shard_map/bkgqs,bqkgd->bskd/dot_general | solution.py:448
  226.7 0.8 fusion.36
  227.5 0.8 fusion.35
  228.3 0.8 fusion.34
  229.0 0.8 fusion.33
  230.1 43.5 %shard_map.87 = (f32[64,128]{1,0:T(8,128)S(1)}, f32[64,512]{1,0:T(8,128)S(1)}) custom-call(bf16[2,2,4,2,4,2,32,128]{7,6,5,4,3,2,1,0:T(8,128)(2,1)S(1)} %bitcast.140, bf16[2,2,4,2,4,2,32,512]{7,6,5,4,3,2,1,0:T(8,128)(2,1)} %bitcast.145), custom_call_target="tpu_custom_call" | custom-call | tf_op jit(solution)/shard_map/pallas_call | solution.py:346
  273.5 0.6 copy.72
  274.1 0.7 copy.73
  (35 shorter events, 0.8 us)
Async XLA Ops:
  0.6 2.9 %copy-start.11 = (bf16[2048]{0:T(1024)(128)(2,1)S(1)}, bf16[2048]{0:T(1024)(128)(2,1)}, u32[]{:S(2)}) copy-start(bf16[2048]{0:T(1024)(128)(2,1)} %param.8) | copy-start | bytes 12292
  1.3 4.1 %copy-start.5 = (bf16[512,2048]{1,0:T(8,128)(2,1)S(1)}, bf16[512,2048]{1,0:T(8,128)(2,1)}, u32[]{:S(2)}) copy-start(bf16[512,2048]{1,0:T(8,128)(2,1)} %param.7) | copy-start | bytes 6291460
  6.0 5.4 %copy-start = (bf16[64,2048]{1,0:T(8,128)(2,1)S(1)}, bf16[64,2048]{1,0:T(8,128)(2,1)}, u32[]{:S(2)}) copy-start(bf16[64,2048]{1,0:T(8,128)(2,1)} %param.9) | copy-start | bytes 786436
  6.0 5.3 %copy-start.1 = (bf16[64,2048]{1,0:T(8,128)(2,1)S(1)}, bf16[64,2048]{1,0:T(8,128)(2,1)}, u32[]{:S(2)}) copy-start(bf16[64,2048]{1,0:T(8,128)(2,1)} %param.12) | copy-start | bytes 786436
  6.0 5.3 %copy-start.2 = (bf16[64,512]{1,0:T(8,128)(2,1)S(1)}, bf16[64,512]{1,0:T(8,128)(2,1)}, u32[]{:S(2)}) copy-start(bf16[64,512]{1,0:T(8,128)(2,1)} %param.10) | copy-start | bytes 196612
  6.0 5.3 %copy-start.3 = (bf16[64,512]{1,0:T(8,128)(2,1)S(1)}, bf16[64,512]{1,0:T(8,128)(2,1)}, u32[]{:S(2)}) copy-start(bf16[64,512]{1,0:T(8,128)(2,1)} %param.11) | copy-start | bytes 196612
  125.2 3.8 %copy-start.6 = (f32[512,64]{1,0:T(8,128)S(1)}, f32[512,64]{1,0:T(8,128)}, u32[]{:S(2)}) copy-start(f32[512,64]{1,0:T(8,128)} %get-tuple-element.19) | copy-start | bytes 393220
  148.3 3.1 %copy-start.10 = (bf16[2,256,4,128]{1,0,3,2:T(2,128)(2,1)S(1)}, bf16[2,256,4,128]{1,0,3,2:T(2,128)(2,1)}, u32[]{:S(2)}) copy-start(bf16[2,256,4,128]{1,0,3,2:T(2,128)(2,1)} %convert_element_type.155) | copy-start | bytes 1572868
  149.4 2.0 copy-start.4
  157.9 4.6 %copy-start.9 = (bf16[2,256,4,128]{3,2,1,0:T(4,128)(2,1)S(1)}, bf16[2,256,4,128]{3,2,1,0:T(4,128)(2,1)}, u32[]{:S(2)}) copy-start(bf16[2,256,4,128]{3,2,1,0:T(4,128)(2,1)} %reshape.152) | copy-start | bytes 1572868
  175.8 4.2 %copy-start.8 = (bf16[512,2048]{1,0:T(8,128)(2,1)S(1)}, bf16[512,2048]{1,0:T(8,128)(2,1)}, u32[]{:S(2)}) copy-start(bf16[512,2048]{1,0:T(8,128)(2,1)} %convert_element_type.154) | copy-start | bytes 6291460
  185.8 2.3 copy-start.7

commit v2 on v1

v2 whole, which is shorter than its diff:
```python
import jax
import jax.numpy as jnp
import numpy as np
from jax import lax
from jax.experimental import pallas as pl
from jax.experimental.pallas import tpu as pltpu
from jax.sharding import PartitionSpec as P

MESH = pl.DeviceIdType.MESH
HEAD_DIM = 128
SEQ = 256
norm_eps = 1e-05
rope_base = 500000.0


class Place:
    def __init__(self):
        p = lax.axis_index("probe")
        f = lax.axis_index("fsdp")
        self.p, self.f = p, f
        self.x = lax.rem(f, 4)
        self.zl = lax.rem(lax.div(f, 4), 2)
        self.y = lax.div(f, 8)
        self.zh = lax.div(p, 2)
        self.c = lax.rem(p, 2)
        self.z = self.zh * 2 + self.zl

    def move(self, axis, step):
        x, y, z = self.x, self.y, self.z
        if axis == "x":
            x = lax.rem(x + step + 4, 4)
        elif axis == "y":
            y = lax.rem(y + step + 4, 4)
        else:
            z = lax.rem(z + step + 4, 4)
        return (lax.div(z, 2) * 2 + self.c, y * 8 + lax.rem(z, 2) * 4 + x)

    def partner(self):
        return (self.zh * 2 + 1 - self.c, self.f)

    def neighbours(self):
        return [self.move(a, s) for a in ("x", "y", "z") for s in (1, -1)] + [self.partner()]


def meet(place):
    barrier = pltpu.get_barrier_semaphore()
    peers = place.neighbours()
    for peer in peers:
        pl.semaphore_signal(barrier, inc=1, device_id=peer, device_id_type=MESH)
    pl.semaphore_wait(barrier, len(peers))


class Copies:
    def __init__(self, send_sems, recv_sems):
        self.send_sems, self.recv_sems = send_sems, recv_sems
        self.used = 0
        self.started = []

    def slot(self):
        self.used += 1
        return self.used - 1

    def send(self, slot, ref, peer, dst=None):
        copy = pltpu.make_async_remote_copy(
            src_ref=ref,
            dst_ref=ref if dst is None else dst,
            send_sem=self.send_sems.at[slot],
            recv_sem=self.recv_sems.at[slot],
            device_id=peer,
            device_id_type=MESH,
        )
        copy.start()
        self.started.append(copy)

    def wait_recv(self, slot, ref, peer):
        pltpu.make_async_remote_copy(
            src_ref=ref,
            dst_ref=ref,
            send_sem=self.send_sems.at[slot],
            recv_sem=self.recv_sems.at[slot],
            device_id=peer,
            device_id_type=MESH,
        ).wait_recv()

    def finish(self):
        for copy in self.started:
            copy.wait_send()


def gather_steps(buf, order, place, copies):
    def region(have, where, core, halves):
        def pick(axis, extent):
            return pl.ds(0, extent) if axis in have else pl.ds(where[axis], 1)

        return buf.at[pick("y", 4), pick("z", 2), pick("x", 4), core, halves]

    here = {"x": place.x, "y": place.y, "z": place.zl}
    core, other = place.c, 1 - place.c
    partner = place.partner()
    from_partner = []

    def share(have, where):
        slot = copies.slot()
        copies.send(slot, region(have, where, core, pl.ds(0, 2)), partner)
        from_partner.append((slot, region(have, where, other, pl.ds(0, 2))))

    have = ()
    for phase, axis in enumerate(order):
        last = phase == 2
        if last:
            share(have, here)
        if axis == "z":
            slots = (copies.slot(), copies.slot())
            for half, step in ((0, 1), (1, -1)):
                copies.send(
                    slots[half], region(have, here, core, pl.ds(half, 1)), place.move("z", step)
                )
            there = dict(here, z=1 - place.zl)
            for half, step in ((0, -1), (1, 1)):
                yield
                copies.wait_recv(
                    slots[half], region(have, there, core, pl.ds(half, 1)), place.move("z", step)
                )
            if last:
                share(have, there)
        else:
            at = {s: dict(here, **{axis: lax.rem(here[axis] + s + 4, 4)}) for s in (-1, 1, 2)}
            up, down, up2, down2 = (copies.slot() for _ in range(4))
            ahead, behind = place.move(axis, 1), place.move(axis, -1)
            copies.send(up, region(have, here, core, pl.ds(0, 2)), ahead)
            copies.send(down, region(have, here, core, pl.ds(0, 2)), behind)
            yield
            copies.wait_recv(up, region(have, at[-1], core, pl.ds(0, 2)), behind)
            copies.send(up2, region(have, at[-1], core, pl.ds(0, 1)), ahead)
            if last:
                share(have, at[-1])
            yield
            copies.wait_recv(down, region(have, at[1], core, pl.ds(0, 2)), ahead)
            copies.send(down2, region(have, at[1], core, pl.ds(1, 1)), behind)
            if last:
                share(have, at[1])
            yield
            copies.wait_recv(up2, region(have, at[2], core, pl.ds(0, 1)), behind)
            yield
            copies.wait_recv(down2, region(have, at[2], core, pl.ds(1, 1)), ahead)
            if last:
                share(have, at[2])
        have = have + (axis,)
    for slot, ref in from_partner:
        yield
        copies.wait_recv(slot, ref, partner)


def in_turn(walks):
    walks = list(walks)
    while walks:
        left = []
        for walk in walks:
            try:
                next(walk)
                left.append(walk)
            except StopIteration:
                pass
        walks = left


def wrap32(value):
    value &= 0xFFFFFFFF
    return value - (1 << 32) if value >= 1 << 31 else value


MIX = 747796405


def fill_signs(dst, seed, code, table_columns, first_row, row_total, first_column):
    width = dst.shape[1]
    step = 32
    lanes = lax.broadcasted_iota(jnp.int32, (step, width), 1)
    tile = (lax.broadcasted_iota(jnp.int32, (step, width), 0) * table_columns + lanes) * MIX
    base = seed * 1664525 + wrap32(code * 374761393 + first_column * MIX)

    def one(i, carry):
        row = first_row + i * step
        hashed = tile + (base + row * wrap32(table_columns * MIX))
        hashed = hashed ^ lax.shift_right_logical(hashed, jnp.int32(15))
        hashed = hashed * 668265261
        hashed = hashed ^ lax.shift_right_logical(hashed, jnp.int32(13))
        hashed = hashed * 1274126177
        hashed = hashed ^ lax.shift_right_logical(hashed, jnp.int32(16))
        signs = jnp.where((hashed & 1) == 1, jnp.float32(1.0), jnp.float32(-1.0))
        dst[pl.ds(pl.multiple_of(row, step), step), :] = signs.astype(jnp.bfloat16)
        return carry

    lax.fori_loop(0, row_total // step, one, 0)


def dot(a, b):
    return jnp.dot(a, b, preferred_element_type=jnp.float32)


def dot_t(a, b):
    return lax.dot_general(a, b, (((1,), (1,)), ((), ())), preferred_element_type=jnp.float32)


def front_kernel(
    seed_ref, hidden, gain, turns, wq, wk, wv, wo,
    normed_t, context_t, cotangent_u, back_value,
    qkv, out, normed, signs, tangent, query, key, value, weights, context, tangent_context, part,
    cotangent, send_sems, recv_sems, load_sems,
):
    place = Place()
    bf16 = jnp.bfloat16
    loads = []

    def load(src, dst):
        copy = pltpu.make_async_copy(src, dst, load_sems.at[len(loads)])
        copy.start()
        loads.append(copy)

    def own(buf, columns):
        return buf.at[place.y, place.zl, place.x, place.c, :, :, columns]

    def rows(w, columns):
        return w.at[place.c, :, :, columns]

    for h in range(4):
        load(rows(wq, pl.ds(h * 512, 512)), own(qkv.at[h], pl.ds(0, 512)))
        load(rows(wk, pl.ds(h * 128, 128)), own(qkv.at[h], pl.ds(512, 128)))
        load(rows(wv, pl.ds(h * 128, 128)), own(qkv.at[h], pl.ds(640, 128)))
    for j in range(4):
        load(rows(wo, pl.ds(j * 512, 512)), own(out.at[j], pl.ds(0, 512)))
    meet(place)
    for copy in loads:
        copy.wait()
    copies = Copies(send_sems, recv_sems)
    seed = seed_ref[0]

    def norm(i):
        at = pl.ds(128 * i, 128)
        x = hidden[at, :].astype(jnp.float32)
        inverse = lax.rsqrt(jnp.mean(x * x, axis=1, keepdims=True) + norm_eps)
        n = (x * inverse * gain[...].astype(jnp.float32)).astype(bf16)
        normed[at, :] = n
        normed_t[:, at] = n.T

    def tangents(i):
        table = signs.at[0, :, pl.ds(256 * i, 256)]
        fill_signs(table, seed, 0, 512, 0, 2048, 256 * i)
        tangent[:, pl.ds(256 * i, 256)] = (dot(normed[...], table[...]) * 2048**-0.5).astype(bf16)

    def sign_part(i):
        fill_signs(signs.at[i // 2], seed, 1, 2048, 1024 * (i % 2), 1024, 512 * (i // 2))

    def project(h):
        cosine = jnp.concatenate([turns[0], turns[0]], 0)
        sine = jnp.concatenate([turns[1], turns[1]], 0)

        def rope(x):
            return (x * cosine + pltpu.roll(x, 64, 1) * sine).astype(bf16)

        for block in range(3):
            table = qkv[h, :, :, :, :, :, :, pl.ds(256 * block, 256)].reshape(2048, 256)
            raw = dot(normed[...], table)
            left, right = raw[:, :128], raw[:, 128:]
            if block < 2:
                query[2 * block] = rope(left)
                query[2 * block + 1] = rope(right)
            else:
                key[...] = rope(left)
                value[:, pl.ds(0, 128)] = right.astype(bf16)
                value[:, pl.ds(128, 128)] = tangent[:, pl.ds(128 * h, 128)]

    def attend(h, g):
        causal = lax.broadcasted_iota(jnp.int32, (SEQ, SEQ), 0) >= lax.broadcasted_iota(
            jnp.int32, (SEQ, SEQ), 1
        )
        head = pl.ds(128 * (4 * h + g), 128)
        for s in range(2):
            at = pl.ds(SEQ * s, SEQ)
            scores = dot_t(query[g, at, :], key[at, :]) * HEAD_DIM**-0.5
            scores = jnp.where(causal, scores, -1e30)
            raised = jnp.exp(scores - jnp.max(scores, axis=1, keepdims=True))
            chances = (raised * (1.0 / jnp.sum(raised, axis=1, keepdims=True))).astype(bf16)
            weights[h, s, g] = chances
            mixed = dot(chances, value[at, :]).astype(bf16)
            context[at, head] = mixed[:, :128]
            tangent_context[at, head] = mixed[:, 128:]
            context_t[head, at] = mixed[:, :128].T

    def probe(j):
        for block in range(2):
            at = pl.ds(256 * block, 256)
            part[j, :, at] = dot(context[...], signs[j, :, at]) * 2048**-0.5

    def forward(j):
        for block in range(2):
            at = pl.ds(256 * block, 256)
            table = out[j, :, :, :, :, :, :, at].reshape(2048, 256)
            total = (dot(tangent_context[...], table) + part[j, :, at]).astype(bf16)
            cotangent[:, pl.ds(512 * j + 256 * block, 256)] = total
            for side in range(2):
                cotangent_u[2 * block + side, :, pl.ds(128 * j, 128)] = total[
                    :, 128 * side : 128 * side + 128
                ]

    def back(h):
        table = jnp.concatenate([out[j, h].reshape(512, 512) for j in range(4)], 1)
        for s in range(2):
            at = pl.ds(SEQ * s, SEQ)
            turned = dot_t(table, cotangent[at, :]).astype(bf16)
            wide_row = jnp.concatenate([turned[128 * g : 128 * g + 128] for g in range(4)], 1)
            spread = dot(wide_row, weights[h, s].reshape(1024, SEQ)).astype(bf16)
            back_value[at, pl.ds(128 * h, 128)] = spread.T

    walks = [gather_steps(qkv.at[h], GATHER_ORDERS[h], place, copies) for h in range(4)]
    walks += [gather_steps(out.at[j], GATHER_ORDERS[j], place, copies) for j in range(4)]
    tasks = dict(n=norm, t=tangents, s=sign_part, q=project, a=attend, p=probe, f=forward, b=back)
    for what, *where in SCHEDULE:
        if what == "w":
            next(walks[where[0]], None)
        else:
            tasks[what](*where)
    copies.finish()


def front(seed, hidden, gain, turns, wq, wk, wv, wo):
    bf16 = jnp.bfloat16
    halves = [w.reshape(2, 2, 16, w.shape[1]) for w in (wq, wk, wv, wo)]
    copies = 120
    anywhere = pl.BlockSpec(memory_space=pl.ANY)
    vmem = pl.BlockSpec(memory_space=pltpu.VMEM)
    shapes = [(2048, 512), (2048, 512), (4, 512, 512), (512, 512)]
    scratch = [
        (4, 4, 2, 4, 2, 2, 16, 768),
        (4, 4, 2, 4, 2, 2, 16, 512),
        (512, 2048),
        (4, 2048, 512),
        (512, 512),
        (4, 512, 128),
        (512, 128),
        (512, 256),
        (4, 2, 4, SEQ, SEQ),
        (512, 2048),
        (512, 2048),
    ]
    return pl.pallas_call(
        front_kernel,
        out_shape=[jax.ShapeDtypeStruct(s, bf16) for s in shapes],
        in_specs=[pl.BlockSpec(memory_space=pltpu.SMEM)] + [vmem] * 3 + [anywhere] * 4,
        out_specs=[vmem] * 4,
        scratch_shapes=[pltpu.VMEM(s, bf16) for s in scratch]
        + [
            pltpu.VMEM((4, 512, 512), jnp.float32),
            pltpu.VMEM((512, 2048), bf16),
            pltpu.SemaphoreType.DMA((copies,)),
            pltpu.SemaphoreType.DMA((copies,)),
            pltpu.SemaphoreType.DMA((16,)),
        ],
        compiler_params=pltpu.CompilerParams(
            collective_id=0, has_side_effects=True, vmem_limit_bytes=63 * 1024 * 1024
        ),
    )(seed, hidden, gain.reshape(1, -1), turns, *halves)


def turn_tables():
    exponent = np.arange(64, dtype=np.float64) * (-2.0 / HEAD_DIM)
    angles = np.arange(SEQ, dtype=np.float64)[:, None] * np.power(rope_base, exponent)[None, :]
    cosine, sine = np.cos(angles), np.sin(angles)
    return np.stack(
        [np.concatenate([cosine, cosine], 1), np.concatenate([-sine, sine], 1)]
    ).astype(np.float32)


GATHER_ORDERS = (('x', 'y', 'z'), ('y', 'x', 'z'), ('z', 'x', 'y'), ('z', 'y', 'x'))
SCHEDULE = (
    ('w', 0),
    ('w', 1),
    ('w', 2),
    ('w', 3),
    ('w', 4),
    ('n', 0),
    ('n', 1),
    ('n', 2),
    ('n', 3),
    ('w', 2),
    ('w', 2),
    ('w', 0),
    ('w', 0),
    ('w', 1),
    ('w', 1),
    ('w', 3),
    ('w', 3),
    ('t', 0),
    ('w', 4),
    ('w', 4),
    ('w', 1),
    ('w', 1),
    ('t', 1),
    ('w', 0),
    ('w', 0),
    ('w', 2),
    ('w', 2),
    ('w', 3),
    ('w', 3),
    ('w', 4),
    ('w', 4),
    ('s', 0),
    ('s', 1),
    ('s', 2),
    ('w', 1),
    ('w', 1),
    ('s', 3),
    ('w', 2),
    ('w', 2),
    ('w', 0),
    ('w', 0),
    ('s', 4),
    ('w', 3),
    ('w', 3),
    ('s', 5),
    ('w', 1),
    ('w', 1),
    ('s', 6),
    ('w', 4),
    ('w', 4),
    ('s', 7),
    ('w', 3),
    ('w', 3),
    ('w', 2),
    ('w', 2),
    ('w', 1),
    ('w', 1),
    ('w', 1),
    ('w', 0),
    ('w', 0),
    ('w', 4),
    ('w', 4),
    ('w', 3),
    ('w', 3),
    ('w', 3),
    ('w', 3),
    ('w', 3),
    ('w', 2),
    ('w', 2),
    ('w', 2),
    ('w', 2),
    ('w', 2),
    ('w', 1),
    ('w', 5),
    ('q', 1),
    ('a', 1, 0),
    ('w', 5),
    ('w', 5),
    ('a', 1, 1),
    ('w', 0),
    ('w', 0),
    ('w', 0),
    ('a', 1, 2),
    ('w', 3),
    ('w', 5),
    ('w', 5),
    ('w', 6),
    ('a', 1, 3),
    ('w', 2),
    ('w', 7),
    ('q', 2),
    ('w', 0),
    ('w', 4),
    ('w', 4),
    ('w', 4),
    ('w', 6),
    ('w', 6),
    ('a', 2, 0),
    ('w', 5),
    ('w', 5),
    ('w', 7),
    ('w', 7),
    ('a', 2, 1),
    ('a', 2, 2),
    ('w', 4),
    ('w', 6),
    ('w', 6),
    ('a', 2, 3),
    ('w', 5),
    ('w', 5),
    ('w', 7),
    ('w', 7),
    ('q', 0),
    ('w', 6),
    ('w', 6),
    ('a', 0, 0),
    ('w', 7),
    ('w', 7),
    ('a', 0, 1),
    ('a', 0, 2),
    ('a', 0, 3),
    ('q', 3),
    ('w', 5),
    ('w', 5),
    ('w', 5),
    ('a', 3, 0),
    ('w', 6),
    ('w', 6),
    ('a', 3, 1),
    ('w', 7),
    ('w', 7),
    ('a', 3, 2),
    ('w', 5),
    ('a', 3, 3),
    ('p', 0),
    ('w', 6),
    ('w', 6),
    ('w', 6),
    ('w', 6),
    ('w', 6),
    ('p', 1),
    ('w', 7),
    ('w', 7),
    ('w', 7),
    ('w', 7),
    ('w', 7),
    ('p', 2),
    ('p', 3),
    ('w', 6),
    ('f', 0),
    ('w', 7),
    ('f', 1),
    ('f', 2),
    ('f', 3),
    ('b', 0),
    ('b', 1),
    ('b', 2),
    ('b', 3),
)


REDUCE_ORDERS = (("x", "y", "z"), ("y", "z", "x"), ("x", "z", "y"), ("y", "x", "z"), ("z", "x", "y"))


def wide(value):
    return value.astype(jnp.float32)


def reduce_steps(fill, order, mine, given, theirs, landing, result, place, copies):
    here = {"x": place.x, "y": place.y, "z": place.z}

    def region(done, where, half):
        at = dict(where)

        def pick(axis, extent):
            return pl.ds(at[axis], 1) if axis in done else pl.ds(0, extent)

        if "z" in done:
            zh, zl = pl.ds(lax.div(at["z"], 2), 1), pl.ds(lax.rem(at["z"], 2), 1)
        else:
            zh, zl = pl.ds(0, 2), pl.ds(0, 2)
        return mine.at[zh, pick("y", 4), zl, pick("x", 4), half]

    fill()
    partner_slot = copies.slot()
    copies.send(partner_slot, given, place.partner(), dst=theirs)
    yield
    copies.wait_recv(partner_slot, theirs, place.partner())

    def add_partner(i, carry):
        zh, y = lax.div(i, 4), lax.rem(i, 4)
        mine[zh, y] = (wide(mine[zh, y]) + wide(theirs[zh, y])).astype(jnp.bfloat16)
        return carry

    lax.fori_loop(0, 8, add_partner, 0)
    done = ()
    for stage, axis in enumerate(order):
        land = landing[stage]
        done = done + (axis,)
        at = {s: dict(here, **{axis: lax.rem(here[axis] + s + 4, 4)}) for s in (-1, 0, 1, 2)}
        ahead, behind = place.move(axis, 1), place.move(axis, -1)
        slots = [copies.slot() for _ in range(6)]

        def send(slot, step, half, peer):
            copies.send(slots[slot], region(done, at[step], half), peer, dst=land.at[slot])

        def wait(slot, peer):
            copies.wait_recv(slots[slot], land.at[slot], peer)

        send(0, 2, 0, ahead)
        send(1, 2, 1, behind)
        send(3, 1, 1, ahead)
        send(4, -1, 0, behind)
        yield
        for slot, step, half, source, peer, onward in (
            (0, 1, 0, behind, ahead, 2),
            (1, -1, 1, ahead, behind, 5),
        ):
            wait(slot, source)
            part = region(done, at[step], half)
            part[...] = (wide(part[...]) + wide(land[slot])).astype(jnp.bfloat16)
            send(onward, step, half, peer)
        yield
        for slot, source in ((3, behind), (4, ahead), (2, behind), (5, ahead)):
            wait(slot, source)
        for half in (0, 1):
            part = region(done, at[0], half)
            total = wide(part[...]) + wide(land[2 + half]) + wide(land[4 + half])
            if stage == 2:
                result[pl.ds(32 * half, 32), :] = total.reshape(32, 128)
            else:
                part[...] = total.astype(jnp.bfloat16)


def stage_shape(order, stage):
    done = order[: stage + 1]
    z = 1 if "z" in done else 2
    return (6, z, 1 if "y" in done else 4, z, 1 if "x" in done else 4, 32, 128)


def reduce_kernel(
    normed_t, context_t, cotangent_u, back_value, value_ref, out_ref, terms, theirs, *rest
):
    landing, (send_sems, recv_sems) = rest[:15], rest[15:]
    place = Place()
    copies = Copies(send_sems, recv_sems)
    meet(place)

    def filler(unit):
        def fill():
            left = normed_t if unit == 4 else context_t
            right = back_value if unit == 4 else cotangent_u.at[unit]

            def one(y, carry):
                rows = left[pl.ds(pl.multiple_of(512 * y, 512), 512), :]
                for zh in range(2):
                    both = dot(rows, right[:, pl.ds(256 * zh, 256)]).astype(jnp.bfloat16)
                    for core in range(2):
                        terms[unit, zh, core, y] = both[:, 128 * core : 128 * core + 128].reshape(
                            2, 4, 2, 32, 128
                        )
                return carry

            lax.fori_loop(0, 4, one, 0)

        return fill

    walks = [
        reduce_steps(
            filler(unit),
            REDUCE_ORDERS[unit],
            terms.at[unit, :, place.c],
            terms.at[unit, :, 1 - place.c],
            theirs.at[unit],
            landing[3 * unit : 3 * unit + 3],
            value_ref if unit == 4 else out_ref.at[:, pl.ds(128 * unit, 128)],
            place,
            copies,
        )
        for unit in range(5)
    ]
    for unit in REDUCE_START:
        next(walks[unit], None)
    in_turn(walks)
    copies.finish()


REDUCE_START = (0, 1, 0, 2, 1, 3, 2, 4, 0, 3, 4)


def reduce_all(normed_t, context_t, cotangent_u, back_value):
    table = (2, 4, 2, 4, 2, 32, 128)
    copies = 5 * 19
    vmem = pl.BlockSpec(memory_space=pltpu.VMEM)
    return pl.pallas_call(
        reduce_kernel,
        out_shape=[
            jax.ShapeDtypeStruct((64, 128), jnp.float32),
            jax.ShapeDtypeStruct((64, 512), jnp.float32),
        ],
        in_specs=[vmem] * 4,
        out_specs=[vmem] * 2,
        scratch_shapes=[
            pltpu.VMEM((5, 2, 2) + table[1:], jnp.bfloat16),
            pltpu.VMEM((5,) + table, jnp.bfloat16),
        ]
        + [
            pltpu.VMEM(stage_shape(REDUCE_ORDERS[unit], stage), jnp.bfloat16)
            for unit in range(5)
            for stage in range(3)
        ]
        + [pltpu.SemaphoreType.DMA((copies,)), pltpu.SemaphoreType.DMA((copies,))],
        compiler_params=pltpu.CompilerParams(
            collective_id=1, has_side_effects=True, vmem_limit_bytes=48 * 1024 * 1024
        ),
    )(normed_t, context_t, cotangent_u, back_value)


def body(hidden, norm_gain, query_weight, key_weight, value_weight, output_weight, probe_seed):
    parts = front(
        probe_seed,
        hidden,
        norm_gain,
        jnp.asarray(turn_tables()),
        query_weight,
        key_weight,
        value_weight,
        output_weight,
    )
    return tuple(reduce_all(*parts))


def solution(mesh):
    return jax.shard_map(
        body,
        mesh=mesh,
        in_specs=(
            P(("probe", "fsdp"), None),
            P(),
            P("fsdp", None),
            P("fsdp", None),
            P("fsdp", None),
            P("fsdp", None),
            P("probe"),
        ),
        out_specs=(P("fsdp", "probe"), P("fsdp", "probe")),
        check_vma=False,
    )
```

time: 280 us -> 155 us (0.55); the launches traced: 275 us -> 155 us
  matrix products: 81.4 us -> 0 us
  local copies, waits for them, and re-layouts: 48.4 us -> 6.78 us
  Pallas kernels: 116 us -> 147 us
  other arithmetic: 27.6 us -> 0 us
    dot_general x34 -> x0, matrix products: 81.4 us -> none  [the longest x1 13.5 us: body(): probe_part = jnp.dot(context, signs_out, **f32) * query_width ** (-0.5)]
    pallas_call x1, Pallas kernels: 72.2 us -> 97.6 us  [front(): pl.pallas_call(front_kernel, out_shape=[jax.ShapeDtypeStruct(s, bf16) for...]
    convert_element_type x6 -> x0, local copies, waits for them, and re-layouts: 19.2 us -> none  [the longest x2 9.06 us: body(): context = mix_values(attention, value_rows).astype(jnp.bfloat16)]
    another operation x4 -> x0, other arithmetic: 10.5 us -> none
    unnamed x31 -> x8, local copies, waits for them, and re-layouts: 14.7 us -> 5.49 us
    sub x1 -> x0, other arithmetic: 8.96 us -> none  [attend(): raised = jnp.exp(scores - highest)]
    slice x3 -> x0, local copies, waits for them, and re-layouts: 7.97 us -> none  [the longest x1 4.18 us: body(): out_tables[j]]
    pallas_call x1, Pallas kernels: 43.5 us -> 49.3 us  [reduce_all(): pl.pallas_call(reduce_kernel, out_shape=[jax.ShapeDtypeStruct((64, 128),...]
where the time goes in v2:
time: 155 us
  Pallas kernels  147 us (95%)
  local copies, waits for them, and re-layouts  6.78 us (4%)
    pallas_call x1, Pallas kernels, front(): pl.pallas_call(front_kernel, out_shape=[jax.ShapeDtypeStruct(s, bf16) for...  97.6 us
    pallas_call x1, Pallas kernels, reduce_all(): pl.pallas_call(reduce_kernel, out_shape=[jax.ShapeDtypeStruct((64, 128),...  49.3 us
    unnamed x8, local copies, waits for them, and re-layouts  5.49 us

profile of v2, /device:TPU:0, one launch (start us, length us, event | category | flops | bytes accessed | tf_op | source)
XLA Modules:
  0.0 154.9 jit_solution(15148155744115388978)
XLA Ops:
  1.3 1.3 reshape.19.gain
  2.6 97.6 %shard_map.95 = (bf16[2048,512]{1,0:T(8,128)(2,1)}, bf16[2048,512]{1,0:T(8,128)(2,1)}, bf16[4,512,512]{2,1,0:T(8,128)(2,1)}, bf16[512,512]{1,0:T(8,128)(2,1)}) custom-call(s32[1]{0:T(128)S(6)} %copy.12.seed_ref, bf16[512,2048]{1,0:T(8,128)(2,1)} %hidden.1, bf16[1,2048]{1,0:T(2,128)(2,1)} %reshape.19.gain, f32[2,256,128]{2,1,0:T(8,128)} %constant.2.clone.turns, ...), custom_call_target="tpu_custom_call" | custom-call | tf_op jit(solution)/shard_map/pallas_call | solution.py:346
  100.2 0.0 copy-start
  100.2 1.6 %copy-done = bf16[2048,512]{1,0:T(8,128)(2,1)S(1)} copy-done((bf16[2048,512]{1,0:T(8,128)(2,1)S(1)}, bf16[2048,512]{1,0:T(8,128)(2,1)}, u32[]{:S(2)}) %copy-start) | copy-done | bytes 2097176
  101.8 0.0 copy-start.1
  101.8 1.6 %copy-done.1 = bf16[2048,512]{1,0:T(8,128)(2,1)S(1)} copy-done((bf16[2048,512]{1,0:T(8,128)(2,1)S(1)}, bf16[2048,512]{1,0:T(8,128)(2,1)}, u32[]{:S(2)}) %copy-start.1) | copy-done | bytes 2097176
  103.3 0.0 copy-start.2
  103.3 1.0 copy-done.2
  104.4 49.3 %shard_map.96 = (f32[64,128]{1,0:T(8,128)S(1)}, f32[64,512]{1,0:T(8,128)S(1)}) custom-call(bf16[2048,512]{1,0:T(8,128)(2,1)S(1)} %copy-done, bf16[2048,512]{1,0:T(8,128)(2,1)S(1)} %copy-done.1, bf16[4,512,512]{2,1,0:T(8,128)(2,1)} %get-tuple-element.8.cotangent_u, bf16[512,512]{1,0:T(8,128)(2,1)S(1)} %copy-done.2), custom_call_target="tpu_custom_call" | custom-call | tf_op jit(solution)/shard_map/pallas_call | solution.py:670
  153.7 0.6 copy.13
  154.3 0.7 copy.14
Async XLA Ops:
  100.2 1.6 %copy-start = (bf16[2048,512]{1,0:T(8,128)(2,1)S(1)}, bf16[2048,512]{1,0:T(8,128)(2,1)}, u32[]{:S(2)}) copy-start(bf16[2048,512]{1,0:T(8,128)(2,1)} %get-tuple-element.6.normed_t) | copy-start | bytes 6291460
  101.8 1.6 %copy-start.1 = (bf16[2048,512]{1,0:T(8,128)(2,1)S(1)}, bf16[2048,512]{1,0:T(8,128)(2,1)}, u32[]{:S(2)}) copy-start(bf16[2048,512]{1,0:T(8,128)(2,1)} %get-tuple-element.7.context_t) | copy-start | bytes 6291460
  103.3 1.0 copy-start.2

commit v3 on v2

v3 whole, which is shorter than its diff:
```python
import jax
import jax.numpy as jnp
import numpy as np
from jax import lax
from jax.experimental import pallas as pl
from jax.experimental.pallas import tpu as pltpu
from jax.sharding import PartitionSpec as P

MESH = pl.DeviceIdType.MESH
HEAD_DIM = 128
SEQ = 256
norm_eps = 1e-05
rope_base = 500000.0


class Place:
    def __init__(self):
        p = lax.axis_index("probe")
        f = lax.axis_index("fsdp")
        self.p, self.f = p, f
        self.x = lax.rem(f, 4)
        self.zl = lax.rem(lax.div(f, 4), 2)
        self.y = lax.div(f, 8)
        self.zh = lax.div(p, 2)
        self.c = lax.rem(p, 2)
        self.z = self.zh * 2 + self.zl

    def move(self, axis, step):
        x, y, z = self.x, self.y, self.z
        if axis == "x":
            x = lax.rem(x + step + 4, 4)
        elif axis == "y":
            y = lax.rem(y + step + 4, 4)
        else:
            z = lax.rem(z + step + 4, 4)
        return (lax.div(z, 2) * 2 + self.c, y * 8 + lax.rem(z, 2) * 4 + x)

    def partner(self):
        return (self.zh * 2 + 1 - self.c, self.f)

    def neighbours(self):
        return [self.move(a, s) for a in ("x", "y", "z") for s in (1, -1)] + [self.partner()]


def meet(place):
    barrier = pltpu.get_barrier_semaphore()
    peers = place.neighbours()
    for peer in peers:
        pl.semaphore_signal(barrier, inc=1, device_id=peer, device_id_type=MESH)
    pl.semaphore_wait(barrier, len(peers))


class Copies:
    def __init__(self, send_sems, recv_sems):
        self.send_sems, self.recv_sems = send_sems, recv_sems
        self.used = 0
        self.early = False
        self.started = []

    def slot(self):
        self.used += 1
        return self.used - 1

    def send(self, slot, ref, peer, dst=None):
        copy = pltpu.make_async_remote_copy(
            src_ref=ref,
            dst_ref=ref if dst is None else dst,
            send_sem=self.send_sems.at[slot],
            recv_sem=self.recv_sems.at[slot],
            device_id=peer,
            device_id_type=MESH,
        )
        copy.start()
        self.started.append((self.early, copy))

    def wait_recv(self, slot, ref, peer):
        pltpu.make_async_remote_copy(
            src_ref=ref,
            dst_ref=ref,
            send_sem=self.send_sems.at[slot],
            recv_sem=self.recv_sems.at[slot],
            device_id=peer,
            device_id_type=MESH,
        ).wait_recv()

    def finish(self, early_only=False):
        for early, copy in self.started:
            if early or not early_only:
                copy.wait_send()
        self.started = [s for s in self.started if early_only and not s[0]]


def gather_steps(buf, order, place, copies):
    def region(have, where, core, halves):
        def pick(axis, extent):
            return pl.ds(0, extent) if axis in have else pl.ds(where[axis], 1)

        return buf.at[pick("y", 4), pick("z", 2), pick("x", 4), core, halves]

    here = {"x": place.x, "y": place.y, "z": place.zl}
    core, other = place.c, 1 - place.c
    partner = place.partner()
    from_partner = []

    def share(have, where):
        slot = copies.slot()
        copies.send(slot, region(have, where, core, pl.ds(0, 2)), partner)
        from_partner.append((slot, region(have, where, other, pl.ds(0, 2))))

    have = ()
    for phase, axis in enumerate(order):
        last = phase == 2
        if last:
            share(have, here)
        if axis == "z":
            slots = (copies.slot(), copies.slot())
            for half, step in ((0, 1), (1, -1)):
                copies.send(
                    slots[half], region(have, here, core, pl.ds(half, 1)), place.move("z", step)
                )
            there = dict(here, z=1 - place.zl)
            for half, step in ((0, -1), (1, 1)):
                yield
                copies.wait_recv(
                    slots[half], region(have, there, core, pl.ds(half, 1)), place.move("z", step)
                )
            if last:
                share(have, there)
        else:
            at = {s: dict(here, **{axis: lax.rem(here[axis] + s + 4, 4)}) for s in (-1, 1, 2)}
            up, down, up2, down2 = (copies.slot() for _ in range(4))
            ahead, behind = place.move(axis, 1), place.move(axis, -1)
            copies.send(up, region(have, here, core, pl.ds(0, 2)), ahead)
            copies.send(down, region(have, here, core, pl.ds(0, 2)), behind)
            yield
            copies.wait_recv(up, region(have, at[-1], core, pl.ds(0, 2)), behind)
            copies.send(up2, region(have, at[-1], core, pl.ds(0, 1)), ahead)
            if last:
                share(have, at[-1])
            yield
            copies.wait_recv(down, region(have, at[1], core, pl.ds(0, 2)), ahead)
            copies.send(down2, region(have, at[1], core, pl.ds(1, 1)), behind)
            if last:
                share(have, at[1])
            yield
            copies.wait_recv(up2, region(have, at[2], core, pl.ds(0, 1)), behind)
            yield
            copies.wait_recv(down2, region(have, at[2], core, pl.ds(1, 1)), ahead)
            if last:
                share(have, at[2])
        have = have + (axis,)
    for slot, ref in from_partner:
        yield
        copies.wait_recv(slot, ref, partner)


GATHER_ORDERS = (('y', 'x', 'z'), ('x', 'y', 'z'), ('z', 'y', 'x'), ('x', 'y', 'z'), ('x', 'y', 'z'), ('x', 'y', 'z'), ('y', 'x', 'z'), ('x', 'y', 'z'))
REDUCE_ORDERS = (('z', 'x', 'y'), ('x', 'z', 'y'), ('x', 'y', 'z'), ('x', 'y', 'z'), ('z', 'y', 'x'))
SCHEDULE = (
    ('w', 0),
    ('w', 1),
    ('w', 2),
    ('w', 3),
    ('w', 4),
    ('w', 5),
    ('n', 0),
    ('n', 1),
    ('n', 2),
    ('n', 3),
    ('w', 0),
    ('w', 0),
    ('w', 1),
    ('w', 1),
    ('w', 2),
    ('w', 2),
    ('t', 0),
    ('w', 0),
    ('w', 0),
    ('w', 1),
    ('w', 1),
    ('w', 3),
    ('w', 3),
    ('w', 4),
    ('w', 4),
    ('w', 5),
    ('w', 5),
    ('t', 1),
    ('w', 2),
    ('w', 2),
    ('s', 0),
    ('s', 1),
    ('s', 2),
    ('w', 0),
    ('w', 0),
    ('w', 1),
    ('w', 1),
    ('w', 2),
    ('w', 2),
    ('w', 3),
    ('w', 3),
    ('w', 4),
    ('w', 4),
    ('w', 5),
    ('w', 5),
    ('s', 3),
    ('s', 4),
    ('s', 5),
    ('w', 0),
    ('w', 0),
    ('w', 1),
    ('w', 1),
    ('s', 6),
    ('s', 7),
    ('w', 3),
    ('w', 3),
    ('w', 4),
    ('w', 4),
    ('w', 2),
    ('w', 2),
    ('w', 5),
    ('w', 5),
    ('w', 0),
    ('w', 0),
    ('w', 0),
    ('w', 3),
    ('w', 3),
    ('w', 4),
    ('w', 4),
    ('w', 2),
    ('w', 2),
    ('w', 2),
    ('w', 2),
    ('w', 2),
    ('w', 5),
    ('w', 5),
    ('w', 0),
    ('w', 6),
    ('q', 0),
    ('a', 0, 0),
    ('w', 6),
    ('w', 6),
    ('a', 0, 1),
    ('w', 1),
    ('w', 1),
    ('w', 1),
    ('a', 0, 2),
    ('w', 2),
    ('w', 6),
    ('w', 6),
    ('w', 7),
    ('a', 0, 3),
    ('q', 2),
    ('w', 1),
    ('a', 2, 0),
    ('a', 2, 1),
    ('w', 6),
    ('w', 6),
    ('w', 7),
    ('w', 7),
    ('w', 3),
    ('w', 3),
    ('w', 3),
    ('a', 2, 2),
    ('a', 2, 3),
    ('q', 1),
    ('w', 3),
    ('w', 6),
    ('w', 6),
    ('w', 7),
    ('w', 7),
    ('a', 1, 0),
    ('w', 4),
    ('w', 4),
    ('w', 4),
    ('a', 1, 1),
    ('a', 1, 2),
    ('a', 1, 3),
    ('w', 4),
    ('w', 7),
    ('w', 7),
    ('q', 3),
    ('w', 5),
    ('w', 5),
    ('w', 5),
    ('a', 3, 0),
    ('w', 7),
    ('w', 7),
    ('a', 3, 1),
    ('a', 3, 2),
    ('w', 5),
    ('a', 3, 3),
    ('w', 6),
    ('w', 6),
    ('w', 6),
    ('p', 0),
    ('f', 0),
    ('m', 0),
    ('w', 8),
    ('w', 6),
    ('p', 1),
    ('w', 7),
    ('w', 7),
    ('w', 7),
    ('f', 1),
    ('m', 1),
    ('w', 9),
    ('p', 2),
    ('w', 8),
    ('f', 2),
    ('w', 7),
    ('m', 2),
    ('w', 10),
    ('p', 3),
    ('w', 9),
    ('w', 8),
    ('w', 8),
    ('f', 3),
    ('m', 3),
    ('w', 11),
    ('w', 8),
    ('w', 8),
    ('w', 10),
    ('b', 0),
    ('w', 8),
    ('w', 8),
    ('w', 9),
    ('w', 9),
    ('w', 9),
    ('w', 9),
    ('b', 1),
    ('w', 11),
    ('w', 10),
    ('w', 10),
    ('b', 2),
    ('w', 10),
    ('w', 10),
    ('b', 3),
    ('w', 8),
    ('w', 8),
    ('w', 8),
    ('w', 8),
    ('m', 4),
    ('w', 12),
    ('w', 9),
    ('w', 9),
    ('w', 11),
    ('w', 11),
    ('w', 9),
    ('w', 9),
    ('w', 9),
    ('w', 9),
    ('w', 12),
    ('w', 9),
    ('w', 9),
    ('w', 11),
    ('w', 11),
    ('w', 10),
    ('w', 10),
    ('w', 8),
    ('w', 8),
    ('w', 9),
    ('w', 9),
    ('w', 9),
    ('w', 9),
    ('w', 12),
    ('w', 12),
    ('w', 10),
    ('w', 10),
    ('w', 11),
    ('w', 11),
    ('w', 8),
    ('w', 8),
    ('w', 8),
    ('w', 8),
    ('w', 9),
    ('w', 9),
    ('w', 10),
    ('w', 10),
    ('w', 12),
    ('w', 12),
    ('w', 10),
    ('w', 10),
    ('w', 11),
    ('w', 11),
    ('w', 11),
    ('w', 11),
    ('w', 8),
    ('w', 8),
    ('w', 12),
    ('w', 12),
    ('w', 10),
    ('w', 10),
    ('w', 10),
    ('w', 10),
    ('w', 11),
    ('w', 11),
    ('w', 10),
    ('w', 10),
    ('w', 12),
    ('w', 12),
    ('w', 12),
    ('w', 11),
    ('w', 11),
    ('w', 11),
    ('w', 11),
    ('w', 12),
    ('w', 12),
    ('w', 12),
    ('w', 11),
    ('w', 11),
    ('w', 12),
    ('w', 12),
    ('w', 12),
    ('w', 12),
    ('w', 12),
    ('w', 12),
)


def wide(value):
    return value.astype(jnp.float32)


def reduce_steps(order, table, first_lane, given, theirs, landing, result, place, copies):
    here = {"x": place.x, "y": place.y, "z": place.z}

    def region(done, where, half):
        def pick(axis, extent):
            return pl.ds(where[axis], 1) if axis in done else pl.ds(0, extent)

        zl, lanes = pl.ds(0, 2), pl.ds(first_lane, 256)
        if "z" in done:
            zl = pl.ds(lax.rem(where["z"], 2), 1)
            lanes = pl.ds(pl.multiple_of(first_lane + 128 * lax.div(where["z"], 2), 128), 128)
        return table.at[pick("y", 4), zl, pick("x", 4), half, :, :, lanes]

    partner_slot = copies.slot()
    copies.send(partner_slot, given, place.partner(), dst=theirs)
    yield
    copies.wait_recv(partner_slot, theirs, place.partner())

    def add_partner(y, carry):
        at = (y, slice(None), slice(None), slice(None), slice(None), slice(None), pl.ds(first_lane, 256))
        table[at] = (wide(table[at]) + wide(theirs[y])).astype(jnp.bfloat16)
        return carry

    lax.fori_loop(0, 4, add_partner, 0)
    done = ()
    for stage, axis in enumerate(order):
        land = landing[stage]
        done = done + (axis,)
        at = {s: dict(here, **{axis: lax.rem(here[axis] + s + 4, 4)}) for s in (-1, 0, 1, 2)}
        ahead, behind = place.move(axis, 1), place.move(axis, -1)
        slots = [copies.slot() for _ in range(6)]

        def send(slot, step, half, peer):
            copies.send(slots[slot], region(done, at[step], half), peer, dst=land.at[slot])

        def wait(slot, peer):
            copies.wait_recv(slots[slot], land.at[slot], peer)

        send(0, 2, 0, ahead)
        send(1, 2, 1, behind)
        send(3, 1, 1, ahead)
        send(4, -1, 0, behind)
        for slot, step, half, source, peer, onward in (
            (0, 1, 0, behind, ahead, 2),
            (1, -1, 1, ahead, behind, 5),
        ):
            yield
            wait(slot, source)
            part = region(done, at[step], half)
            part[...] = (wide(part[...]) + wide(land[slot])).astype(jnp.bfloat16)
            send(onward, step, half, peer)
        for slot, source in ((3, behind), (4, ahead), (2, behind), (5, ahead)):
            yield
            wait(slot, source)
        for half in (0, 1):
            part = region(done, at[0], half)
            total = wide(part[...]) + wide(land[2 + half]) + wide(land[4 + half])
            if stage == 2:
                result[pl.ds(32 * half, 32), :] = total.reshape(32, 128)
            else:
                part[...] = total.astype(jnp.bfloat16)


def stage_shape(order, stage):
    done = order[: stage + 1]
    x, y = (1 if axis in done else 4 for axis in "xy")
    zl, lanes = (1, 128) if "z" in done else (2, 256)
    return (6, y, zl, x, 2, 16, lanes)


def wrap32(value):
    value &= 0xFFFFFFFF
    return value - (1 << 32) if value >= 1 << 31 else value


MIX = 747796405


def fill_signs(dst, seed, code, table_columns, first_row, row_total, first_column, spread):
    width = dst.shape[1]
    step = 32
    lanes = lax.broadcasted_iota(jnp.int32, (step, width), 1)
    if spread:
        lanes = lanes + lax.div(lanes, 128) * 384
    tile = (lax.broadcasted_iota(jnp.int32, (step, width), 0) * table_columns + lanes) * MIX
    base = seed * 1664525 + wrap32(code * 374761393 + first_column * MIX)

    def one(i, carry):
        row = first_row + i * step
        hashed = tile + (base + row * wrap32(table_columns * MIX))
        hashed = hashed ^ lax.shift_right_logical(hashed, jnp.int32(15))
        hashed = hashed * 668265261
        hashed = hashed ^ lax.shift_right_logical(hashed, jnp.int32(13))
        hashed = hashed * 1274126177
        hashed = hashed ^ lax.shift_right_logical(hashed, jnp.int32(16))
        signs = jnp.where((hashed & 1) == 1, jnp.float32(1.0), jnp.float32(-1.0))
        dst[pl.ds(pl.multiple_of(row, step), step), :] = signs.astype(jnp.bfloat16)
        return carry

    lax.fori_loop(0, row_total // step, one, 0)


def dot(a, b):
    return jnp.dot(a, b, preferred_element_type=jnp.float32)


def dot_t(a, b):
    return lax.dot_general(a, b, (((1,), (1,)), ((), ())), preferred_element_type=jnp.float32)


def whole_kernel(
    seed_ref, gain, turns, hidden, wq, wk, wv, wo, value_ref, out_ref,
    qkv, out, normed, normed_t, signs, tangent, query, key, value, weights, context, context_t,
    tangent_context, part, cotangent, back_value, theirs, *rest,
):
    landing, (send_sems, recv_sems, load_sems) = rest[:15], rest[15:]
    place = Place()
    bf16 = jnp.bfloat16
    loads = []

    def load(src, dst):
        copy = pltpu.make_async_copy(src, dst, load_sems.at[len(loads)])
        copy.start()
        loads.append(copy)

    def own(buf, columns):
        return buf.at[place.y, place.zl, place.x, place.c, :, :, columns]

    def rows(w, columns):
        return w.at[place.c, :, :, columns]

    for h in range(4):
        load(rows(wq, pl.ds(h * 512, 512)), own(qkv.at[h], pl.ds(0, 512)))
        load(rows(wk, pl.ds(h * 128, 128)), own(qkv.at[h], pl.ds(512, 128)))
        load(rows(wv, pl.ds(h * 128, 128)), own(qkv.at[h], pl.ds(640, 128)))
    for j in range(4):
        for p in range(4):
            load(rows(wo, pl.ds(512 * p + 128 * j, 128)), own(out.at[j], pl.ds(128 * p, 128)))
    load(hidden, normed)
    meet(place)
    for copy in loads:
        copy.wait()
    copies = Copies(send_sems, recv_sems)
    seed = seed_ref[0]

    def norm(i):
        at = pl.ds(128 * i, 128)
        x = normed[at, :].astype(jnp.float32)
        inverse = lax.rsqrt(jnp.mean(x * x, axis=1, keepdims=True) + norm_eps)
        n = (x * inverse * gain[...][None, :].astype(jnp.float32)).astype(bf16)
        normed[at, :] = n
        normed_t[:, at] = n.T

    def tangents(i):
        table = signs.at[0, :, pl.ds(256 * i, 256)]
        fill_signs(table, seed, 0, 512, 0, 2048, 256 * i, False)
        tangent[:, pl.ds(256 * i, 256)] = (dot(normed[...], table[...]) * 2048**-0.5).astype(bf16)

    def sign_part(i):
        fill_signs(signs.at[i // 2], seed, 1, 2048, 1024 * (i % 2), 1024, 128 * (i // 2), True)

    def project(h):
        cosine = jnp.concatenate([turns[0], turns[0]], 0)
        sine = jnp.concatenate([turns[1], turns[1]], 0)

        def rope(x):
            return (x * cosine + pltpu.roll(x, 64, 1) * sine).astype(bf16)

        for block in range(3):
            table = qkv[h, :, :, :, :, :, :, pl.ds(256 * block, 256)].reshape(2048, 256)
            raw = dot(normed[...], table)
            left, right = raw[:, :128], raw[:, 128:]
            if block < 2:
                query[2 * block] = rope(left)
                query[2 * block + 1] = rope(right)
            else:
                key[...] = rope(left)
                value[:, pl.ds(0, 128)] = right.astype(bf16)
                value[:, pl.ds(128, 128)] = tangent[:, pl.ds(128 * h, 128)]

    def attend(h, g):
        causal = lax.broadcasted_iota(jnp.int32, (SEQ, SEQ), 0) >= lax.broadcasted_iota(
            jnp.int32, (SEQ, SEQ), 1
        )
        head = pl.ds(128 * (4 * h + g), 128)
        for s in range(2):
            at = pl.ds(SEQ * s, SEQ)
            scores = dot_t(query[g, at, :], key[at, :]) * HEAD_DIM**-0.5
            scores = jnp.where(causal, scores, -1e30)
            raised = jnp.exp(scores - jnp.max(scores, axis=1, keepdims=True))
            chances = (raised * (1.0 / jnp.sum(raised, axis=1, keepdims=True))).astype(bf16)
            weights[h, s, g] = chances
            mixed = dot(chances, value[at, :]).astype(bf16)
            context[at, head] = mixed[:, :128]
            tangent_context[at, head] = mixed[:, 128:]
            context_t[head, at] = mixed[:, :128].T

    def probe(j):
        for block in range(2):
            at = pl.ds(256 * block, 256)
            part[j, :, at] = (dot(context[...], signs[j, :, at]) * 2048**-0.5).astype(bf16)

    def forward(j):
        for block in range(2):
            at = pl.ds(256 * block, 256)
            table = out[j, :, :, :, :, :, :, at].reshape(2048, 256)
            total = (dot(tangent_context[...], table) + part[j, :, at].astype(jnp.float32)).astype(bf16)
            cotangent[:, pl.ds(512 * j + 256 * block, 256)] = total

    def back(h):
        table = jnp.concatenate([out[j, h].reshape(512, 512) for j in range(4)], 1)
        for s in range(2):
            at = pl.ds(SEQ * s, SEQ)
            turned = dot_t(table, cotangent[at, :]).astype(bf16)
            wide_row = jnp.concatenate([turned[128 * g : 128 * g + 128] for g in range(4)], 1)
            spread = dot(wide_row, weights[h, s].reshape(1024, SEQ)).astype(bf16)
            back_value[at, pl.ds(128 * h, 128)] = spread.T

    def own_term(unit, zh, core):
        side = lax.rem(place.c + core, 2)
        if unit == 4:
            return side, pl.ds(512 + 128 * zh, 128)
        return unit, pl.ds(pl.multiple_of(256 * side + 128 * zh, 128), 128)

    def terms(unit):
        if unit == TERM_FIRST:
            copies.finish(early_only=True)
        left = normed_t if unit == 4 else context_t

        def one(y, carry):
            rows = left[pl.ds(pl.multiple_of(512 * y, 512), 512), :]
            for zh in range(2):
                if unit == 4:
                    right = back_value[:, pl.ds(256 * zh, 256)]
                else:
                    right = cotangent[:, pl.ds(512 * unit + 256 * zh, 256)]
                both = dot(rows, right).astype(bf16)
                for core in range(2):
                    h, lanes = own_term(unit, zh, core)
                    qkv[h, y, :, :, :, :, :, lanes] = both[:, 128 * core : 128 * core + 128].reshape(
                        2, 4, 2, 2, 16, 128
                    )
            return carry

        lax.fori_loop(0, 4, one, 0)

    def reduce_walk(unit):
        mine = (0, 512) if unit == 4 else (unit, 0)
        given = qkv.at[1, :, :, :, :, :, :, pl.ds(512, 256)]
        if unit < 4:
            given = qkv.at[unit, :, :, :, :, :, :, pl.ds(256, 256)]
        return reduce_steps(
            REDUCE_ORDERS[unit],
            qkv.at[mine[0]],
            mine[1],
            given,
            theirs.at[unit],
            landing[3 * unit : 3 * unit + 3],
            value_ref if unit == 4 else out_ref.at[:, pl.ds(128 * unit, 128)],
            place,
            copies,
        )

    walks = [gather_steps(qkv.at[h], GATHER_ORDERS[h], place, copies) for h in range(4)]
    walks += [gather_steps(out.at[j], GATHER_ORDERS[4 + j], place, copies) for j in range(4)]
    walks += [reduce_walk(unit) for unit in range(5)]
    tasks = dict(
        n=norm, t=tangents, s=sign_part, q=project, a=attend, p=probe, f=forward, b=back, m=terms
    )
    for what, *where in SCHEDULE:
        if what == "w":
            copies.early = where[0] < 4
            next(walks[where[0]], None)
        else:
            tasks[what](*where)
    copies.finish()


TERM_FIRST = [where[0] for what, *where in SCHEDULE if what == "m"][0]


def whole(seed, hidden, gain, turns, wq, wk, wv, wo):
    bf16 = jnp.bfloat16
    halves = [w.reshape(2, 2, 16, w.shape[1]) for w in (wq, wk, wv, wo)]
    copies = 210
    anywhere = pl.BlockSpec(memory_space=pl.ANY)
    vmem = pl.BlockSpec(memory_space=pltpu.VMEM)
    scratch = [
        (4, 4, 2, 4, 2, 2, 16, 768),
        (4, 4, 2, 4, 2, 2, 16, 512),
        (512, 2048),
        (2048, 512),
        (4, 2048, 512),
        (512, 512),
        (4, 512, 128),
        (512, 128),
        (512, 256),
        (4, 2, 4, SEQ, SEQ),
        (512, 2048),
        (2048, 512),
        (512, 2048),
    ]
    landings = [stage_shape(REDUCE_ORDERS[u], stage) for u in range(5) for stage in range(3)]
    scratch += [(4, 512, 512), (512, 2048), (512, 512), (5, 4, 2, 4, 2, 2, 16, 256)] + landings
    return pl.pallas_call(
        whole_kernel,
        out_shape=[
            jax.ShapeDtypeStruct((64, 128), jnp.float32),
            jax.ShapeDtypeStruct((64, 512), jnp.float32),
        ],
        in_specs=[pl.BlockSpec(memory_space=pltpu.SMEM)] + [vmem] * 2 + [anywhere] * 5,
        out_specs=[vmem] * 2,
        scratch_shapes=[pltpu.VMEM(s, bf16) for s in scratch]
        + [
            pltpu.SemaphoreType.DMA((copies,)),
            pltpu.SemaphoreType.DMA((copies,)),
            pltpu.SemaphoreType.DMA((32,)),
        ],
        compiler_params=pltpu.CompilerParams(
            collective_id=0, has_side_effects=True, vmem_limit_bytes=67043328
        ),
    )(seed, gain, turns, hidden, *halves)


def turn_tables():
    exponent = np.arange(64, dtype=np.float64) * (-2.0 / HEAD_DIM)
    angles = np.arange(SEQ, dtype=np.float64)[:, None] * np.power(rope_base, exponent)[None, :]
    cosine, sine = np.cos(angles), np.sin(angles)
    return np.stack(
        [np.concatenate([cosine, cosine], 1), np.concatenate([-sine, sine], 1)]
    ).astype(np.float32)

def body(hidden, norm_gain, query_weight, key_weight, value_weight, output_weight, probe_seed):
    return tuple(
        whole(
            probe_seed,
            hidden,
            norm_gain,
            jnp.asarray(turn_tables()),
            query_weight,
            key_weight,
            value_weight,
            output_weight,
        )
    )


def solution(mesh):
    return jax.shard_map(
        body,
        mesh=mesh,
        in_specs=(
            P(("probe", "fsdp"), None),
            P(),
            P("fsdp", None),
            P("fsdp", None),
            P("fsdp", None),
            P("fsdp", None),
            P("probe"),
        ),
        out_specs=(P("fsdp", "probe"), P("fsdp", "probe")),
        check_vma=False,
    )
```

time: 155 us -> 143 us (0.923)
  Pallas kernels: 147 us -> 138 us
  local copies, waits for them, and re-layouts: 6.78 us -> 2.94 us
    pallas_call x2 -> x1, Pallas kernels: 147 us -> 138 us  [whole(): pl.pallas_call(whole_kernel, out_shape=[jax.ShapeDtypeStruct((64, 128), j...]
    unnamed x8 -> x2, local copies, waits for them, and re-layouts: 5.49 us -> 2.94 us
where the time goes in v3:
time: 143 us; the launch traced here: 142 us
  Pallas kernels  138 us (97%)
  local copies, waits for them, and re-layouts  2.94 us (2%)
    pallas_call x1, Pallas kernels, whole(): pl.pallas_call(whole_kernel, out_shape=[jax.ShapeDtypeStruct((64, 128), j...  138 us
    unnamed x2, local copies, waits for them, and re-layouts  2.94 us

profile of v3, /device:TPU:0, one launch (start us, length us, event | category | flops | bytes accessed | tf_op | source)
XLA Modules:
  0.0 141.8 jit_solution(15139309720720511224)
XLA Ops:
  1.3 137.6 %shard_map.95 = (f32[64,128]{1,0:T(8,128)}, f32[64,512]{1,0:T(8,128)}) custom-call(s32[1]{0:T(128)S(6)} %copy.12.seed_ref, bf16[2048]{0:T(1024)(128)(2,1)} %gain.1, f32[2,256,128]{2,1,0:T(8,128)} %constant.2.clone.turns, bf16[512,2048]{1,0:T(8,128)(2,1)} %hidden.1, bf16[2,2,16,2048]{3,2,1,0:T(8,128)(2,1)} %bitcast.4, bf16[2,2,16,512]{3,2,1,0:T(8,128)(2,1)} %bitcast.6, ...), custom_call_target="tpu_custom_call" | custom-call | tf_op jit(solution)/shard_map/pallas_call | solution.py:728
  138.8 1.4 copy.13
  140.2 1.6 %copy.14 = f32[64,512]{1,0:T(8,128)} copy(f32[64,512]{1,0:T(8,128)} %get-tuple-element.5) | data formatting | bytes 262144

commit v4 on v3

--- a/solution.py
+++ b/solution.py
@@ -39,15 +39,17 @@
         return (self.zh * 2 + 1 - self.c, self.f)
 
     def neighbours(self):
-        return [self.move(a, s) for a in ("x", "y", "z") for s in (1, -1)] + [self.partner()]
+        return [self.move(a, s) for a in ("x", "y", "z") for s in (1, -1, 2)] + [self.partner()]
+
+
+def greet(place):
+    barrier = pltpu.get_barrier_semaphore()
+    for peer in place.neighbours():
+        pl.semaphore_signal(barrier, inc=1, device_id=peer, device_id_type=MESH)
 
 
 def meet(place):
-    barrier = pltpu.get_barrier_semaphore()
-    peers = place.neighbours()
-    for peer in peers:
-        pl.semaphore_signal(barrier, inc=1, device_id=peer, device_id_type=MESH)
-    pl.semaphore_wait(barrier, len(peers))
+    pl.semaphore_wait(pltpu.get_barrier_semaphore(), len(place.neighbours()))
 
 
 class Copies:
@@ -90,12 +92,12 @@
         self.started = [s for s in self.started if early_only and not s[0]]
 
 
-def gather_steps(buf, order, place, copies):
+def gather_steps(buf, lanes, order, place, copies):
     def region(have, where, core, halves):
         def pick(axis, extent):
             return pl.ds(0, extent) if axis in have else pl.ds(where[axis], 1)
 
-        return buf.at[pick("y", 4), pick("z", 2), pick("x", 4), core, halves]
+        return buf.at[pick("y", 4), pick("z", 2), pick("x", 4), core, halves, :, lanes]
 
     here = {"x": place.x, "y": place.y, "z": place.zl}
     core, other = place.c, 1 - place.c
@@ -126,6 +128,16 @@
                 )
             if last:
                 share(have, there)
+        elif phase == 0:
+            slots = [copies.slot() for _ in range(3)]
+            for slot, step in zip(slots, (-1, 1, 2)):
+                copies.send(slot, region(have, here, core, pl.ds(0, 2)), place.move(axis, step))
+            for slot, step in zip(slots, (1, -1, 2)):
+                yield
+                there = dict(here, **{axis: lax.rem(here[axis] + step + 4, 4)})
+                copies.wait_recv(
+                    slot, region(have, there, core, pl.ds(0, 2)), place.move(axis, step)
+                )
         else:
             at = {s: dict(here, **{axis: lax.rem(here[axis] + s + 4, 4)}) for s in (-1, 1, 2)}
             up, down, up2, down2 = (copies.slot() for _ in range(4))
@@ -154,266 +166,78 @@
         copies.wait_recv(slot, ref, partner)
 
 
-GATHER_ORDERS = (('y', 'x', 'z'), ('x', 'y', 'z'), ('z', 'y', 'x'), ('x', 'y', 'z'), ('x', 'y', 'z'), ('x', 'y', 'z'), ('y', 'x', 'z'), ('x', 'y', 'z'))
-REDUCE_ORDERS = (('z', 'x', 'y'), ('x', 'z', 'y'), ('x', 'y', 'z'), ('x', 'y', 'z'), ('z', 'y', 'x'))
+GATHER_WALKS = (
+    (0, 0, 256, ('y', 'x', 'z')),
+    (0, 256, 256, ('x', 'y', 'z')),
+    (0, 512, 256, ('z', 'x', 'y')),
+    (1, 0, 256, ('y', 'x', 'z')),
+    (1, 256, 256, ('x', 'y', 'z')),
+    (1, 512, 256, ('y', 'z', 'x')),
+    (2, 0, 256, ('y', 'x', 'z')),
+    (2, 256, 256, ('z', 'y', 'x')),
+    (2, 512, 256, ('z', 'x', 'y')),
+    (3, 0, 256, ('z', 'x', 'y')),
+    (3, 256, 256, ('x', 'z', 'y')),
+    (3, 512, 256, ('y', 'x', 'z')),
+    (4, 0, 512, ('y', 'z', 'x')),
+    (5, 0, 512, ('y', 'x', 'z')),
+    (6, 0, 512, ('x', 'z', 'y')),
+    (7, 0, 512, ('y', 'z', 'x')),
+)
+REDUCE_WALKS = (
+    (0, None, ('z', 'y', 'x')),
+    (1, None, ('z', 'y', 'x')),
+    (2, None, ('z', 'x', 'y')),
+    (3, None, ('x', 'z', 'y')),
+    (4, 0, ('x', 'z', 'y')),
+    (4, 1, ('y', 'z', 'x')),
+)
+COPIES = 298
 SCHEDULE = (
-    ('w', 0),
-    ('w', 1),
-    ('w', 2),
-    ('w', 3),
-    ('w', 4),
-    ('w', 5),
-    ('n', 0),
-    ('n', 1),
-    ('n', 2),
-    ('n', 3),
-    ('w', 0),
-    ('w', 0),
-    ('w', 1),
-    ('w', 1),
-    ('w', 2),
-    ('w', 2),
-    ('t', 0),
-    ('w', 0),
-    ('w', 0),
-    ('w', 1),
-    ('w', 1),
-    ('w', 3),
-    ('w', 3),
-    ('w', 4),
-    ('w', 4),
-    ('w', 5),
-    ('w', 5),
-    ('t', 1),
-    ('w', 2),
-    ('w', 2),
-    ('s', 0),
-    ('s', 1),
-    ('s', 2),
-    ('w', 0),
-    ('w', 0),
-    ('w', 1),
-    ('w', 1),
-    ('w', 2),
-    ('w', 2),
-    ('w', 3),
-    ('w', 3),
-    ('w', 4),
-    ('w', 4),
-    ('w', 5),
-    ('w', 5),
-    ('s', 3),
-    ('s', 4),
-    ('s', 5),
-    ('w', 0),
-    ('w', 0),
-    ('w', 1),
-    ('w', 1),
-    ('s', 6),
-    ('s', 7),
-    ('w', 3),
-    ('w', 3),
-    ('w', 4),
-    ('w', 4),
-    ('w', 2),
-    ('w', 2),
-    ('w', 5),
-    ('w', 5),
-    ('w', 0),
-    ('w', 0),
-    ('w', 0),
-    ('w', 3),
-    ('w', 3),
-    ('w', 4),
-    ('w', 4),
-    ('w', 2),
-    ('w', 2),
-    ('w', 2),
-    ('w', 2),
-    ('w', 2),
-    ('w', 5),
-    ('w', 5),
-    ('w', 0),
-    ('w', 6),
-    ('q', 0),
-    ('a', 0, 0),
-    ('w', 6),
-    ('w', 6),
-    ('a', 0, 1),
-    ('w', 1),
-    ('w', 1),
-    ('w', 1),
-    ('a', 0, 2),
-    ('w', 2),
-    ('w', 6),
-    ('w', 6),
-    ('w', 7),
-    ('a', 0, 3),
-    ('q', 2),
-    ('w', 1),
-    ('a', 2, 0),
-    ('a', 2, 1),
-    ('w', 6),
-    ('w', 6),
-    ('w', 7),
-    ('w', 7),
-    ('w', 3),
-    ('w', 3),
-    ('w', 3),
-    ('a', 2, 2),
-    ('a', 2, 3),
-    ('q', 1),
-    ('w', 3),
-    ('w', 6),
-    ('w', 6),
-    ('w', 7),
-    ('w', 7),
-    ('a', 1, 0),
-    ('w', 4),
-    ('w', 4),
-    ('w', 4),
-    ('a', 1, 1),
-    ('a', 1, 2),
-    ('a', 1, 3),
-    ('w', 4),
-    ('w', 7),
-    ('w', 7),
-    ('q', 3),
-    ('w', 5),
-    ('w', 5),
-    ('w', 5),
-    ('a', 3, 0),
-    ('w', 7),
-    ('w', 7),
-    ('a', 3, 1),
-    ('a', 3, 2),
-    ('w', 5),
-    ('a', 3, 3),
-    ('w', 6),
-    ('w', 6),
-    ('w', 6),
-    ('p', 0),
-    ('f', 0),
-    ('m', 0),
-    ('w', 8),
-    ('w', 6),
-    ('p', 1),
-    ('w', 7),
-    ('w', 7),
-    ('w', 7),
-    ('f', 1),
-    ('m', 1),
-    ('w', 9),
-    ('p', 2),
-    ('w', 8),
-    ('f', 2),
-    ('w', 7),
-    ('m', 2),
-    ('w', 10),
-    ('p', 3),
-    ('w', 9),
-    ('w', 8),
-    ('w', 8),
-    ('f', 3),
-    ('m', 3),
-    ('w', 11),
-    ('w', 8),
-    ('w', 8),
-    ('w', 10),
-    ('b', 0),
-    ('w', 8),
-    ('w', 8),
-    ('w', 9),
-    ('w', 9),
-    ('w', 9),
-    ('w', 9),
-    ('b', 1),
-    ('w', 11),
-    ('w', 10),
-    ('w', 10),
-    ('b', 2),
-    ('w', 10),
-    ('w', 10),
-    ('b', 3),
-    ('w', 8),
-    ('w', 8),
-    ('w', 8),
-    ('w', 8),
-    ('m', 4),
-    ('w', 12),
-    ('w', 9),
-    ('w', 9),
-    ('w', 11),
-    ('w', 11),
-    ('w', 9),
-    ('w', 9),
-    ('w', 9),
-    ('w', 9),
-    ('w', 12),
-    ('w', 9),
-    ('w', 9),
-    ('w', 11),
-    ('w', 11),
-    ('w', 10),
-    ('w', 10),
-    ('w', 8),
-    ('w', 8),
-    ('w', 9),
-    ('w', 9),
-    ('w', 9),
-    ('w', 9),
-    ('w', 12),
-    ('w', 12),
-    ('w', 10),
-    ('w', 10),
-    ('w', 11),
-    ('w', 11),
-    ('w', 8),
-    ('w', 8),
-    ('w', 8),
-    ('w', 8),
-    ('w', 9),
-    ('w', 9),
-    ('w', 10),
-    ('w', 10),
-    ('w', 12),
-    ('w', 12),
-    ('w', 10),
-    ('w', 10),
-    ('w', 11),
-    ('w', 11),
-    ('w', 11),
-    ('w', 11),
-    ('w', 8),
-    ('w', 8),
-    ('w', 12),
-    ('w', 12),
-    ('w', 10),
-    ('w', 10),
-    ('w', 10),
-    ('w', 10),
-    ('w', 11),
-    ('w', 11),
-    ('w', 10),
-    ('w', 10),
-    ('w', 12),
-    ('w', 12),
-    ('w', 12),
-    ('w', 11),
-    ('w', 11),
-    ('w', 11),
-    ('w', 11),
-    ('w', 12),
-    ('w', 12),
-    ('w', 12),
-    ('w', 11),
-    ('w', 11),
-    ('w', 12),
-    ('w', 12),
-    ('w', 12),
-    ('w', 12),
-    ('w', 12),
-    ('w', 12),
+    ('s', 2), ('s', 3), ('e',), ('w', 0), ('w', 1), ('w', 2), ('w', 3), ('w', 4), ('w', 5),
+    ('w', 6), ('w', 7), ('w', 8), ('w', 9), ('n', 0), ('n', 1), ('n', 2), ('w', 0), ('w', 0),
+    ('w', 1), ('w', 1), ('w', 2), ('w', 2), ('w', 3), ('w', 4), ('n', 3), ('w', 5), ('w', 6),
+    ('w', 7), ('w', 7), ('w', 8), ('w', 8), ('w', 9), ('w', 9), ('w', 0), ('w', 3), ('w', 4),
+    ('w', 1), ('t', 0), ('w', 2), ('w', 2), ('w', 3), ('w', 4), ('w', 5), ('w', 5), ('w', 6),
+    ('w', 8), ('w', 8), ('t', 1), ('w', 0), ('w', 0), ('w', 1), ('w', 1), ('w', 2), ('w', 2),
+    ('w', 5), ('w', 5), ('w', 6), ('w', 7), ('w', 7), ('w', 9), ('w', 9), ('w', 4), ('w', 4),
+    ('s', 0), ('w', 3), ('w', 3), ('w', 8), ('w', 8), ('s', 1), ('w', 0), ('w', 0), ('w', 1),
+    ('w', 1), ('w', 2), ('w', 2), ('w', 5), ('w', 5), ('w', 7), ('w', 7), ('w', 4), ('w', 4),
+    ('w', 6), ('w', 6), ('w', 9), ('w', 9), ('s', 4), ('w', 0), ('w', 0), ('w', 0), ('w', 3),
+    ('w', 3), ('s', 5), ('w', 5), ('w', 8), ('w', 8), ('w', 5), ('w', 5), ('w', 5), ('w', 5),
+    ('s', 6), ('w', 0), ('w', 1), ('w', 1), ('w', 1), ('w', 2), ('w', 2), ('w', 2), ('w', 2),
+    ('w', 2), ('w', 10), ('s', 7), ('w', 5), ('w', 7), ('w', 7), ('w', 11), ('w', 6), ('w', 6),
+    ('w', 9), ('w', 9), ('w', 10), ('w', 10), ('w', 1), ('w', 12), ('w', 4), ('w', 4), ('w', 4),
+    ('w', 2), ('w', 13), ('q', 0), ('w', 8), ('w', 8), ('w', 8), ('w', 8), ('w', 8), ('w', 10),
+    ('w', 11), ('w', 11), ('w', 7), ('a', 0, 0), ('w', 3), ('w', 3), ('w', 3), ('w', 4), ('w', 7),
+    ('w', 7), ('w', 7), ('w', 7), ('w', 9), ('w', 9), ('w', 9), ('w', 9), ('w', 9), ('w', 11),
+    ('w', 12), ('w', 14), ('a', 0, 1), ('w', 8), ('w', 12), ('w', 13), ('w', 15), ('a', 0, 2),
+    ('w', 3), ('w', 6), ('w', 6), ('w', 6), ('w', 7), ('w', 10), ('w', 10), ('w', 12), ('w', 13),
+    ('w', 9), ('a', 0, 3), ('w', 11), ('w', 11), ('w', 14), ('w', 14), ('w', 15), ('q', 1),
+    ('w', 6), ('w', 13), ('w', 15), ('a', 1, 0), ('w', 11), ('w', 11), ('w', 12), ('w', 12),
+    ('w', 14), ('w', 15), ('a', 1, 1), ('w', 10), ('w', 10), ('a', 1, 2), ('a', 1, 3), ('w', 13),
+    ('w', 13), ('q', 2), ('w', 10), ('w', 10), ('w', 10), ('w', 10), ('w', 10), ('w', 11),
+    ('w', 11), ('w', 11), ('a', 2, 0), ('w', 14), ('w', 14), ('a', 2, 1), ('w', 10), ('w', 15),
+    ('w', 15), ('a', 2, 2), ('w', 11), ('w', 12), ('w', 12), ('a', 2, 3), ('w', 13), ('w', 13),
+    ('q', 3), ('a', 3, 0), ('a', 3, 1), ('w', 14), ('w', 14), ('a', 3, 2), ('w', 15), ('w', 15),
+    ('a', 3, 3), ('p', 0), ('p', 1), ('w', 12), ('w', 12), ('w', 12), ('w', 12), ('w', 12),
+    ('w', 13), ('w', 13), ('w', 13), ('w', 14), ('w', 14), ('w', 14), ('w', 14), ('w', 14),
+    ('p', 2), ('p', 3), ('w', 15), ('w', 15), ('w', 15), ('w', 15), ('w', 15), ('w', 12), ('f', 0),
+    ('m', 0), ('w', 16), ('w', 13), ('w', 14), ('w', 15), ('f', 1), ('m', 1), ('w', 17), ('f', 2),
+    ('m', 2), ('w', 18), ('w', 16), ('f', 3), ('w', 17), ('m', 3), ('w', 19), ('w', 18), ('w', 16),
+    ('w', 16), ('b', 0), ('b', 1), ('w', 16), ('w', 16), ('w', 19), ('b', 2), ('w', 17), ('w', 17),
+    ('b', 3), ('w', 17), ('w', 17), ('m', 4), ('w', 20), ('w', 21), ('w', 18), ('w', 18), ('w', 19),
+    ('w', 19), ('w', 19), ('w', 19), ('w', 18), ('w', 18), ('w', 20), ('w', 21), ('w', 16),
+    ('w', 19), ('w', 16), ('w', 19), ('w', 20), ('w', 20), ('w', 21), ('w', 21), ('w', 17),
+    ('w', 17), ('w', 20), ('w', 20), ('w', 21), ('w', 21), ('w', 16), ('w', 16), ('w', 20),
+    ('w', 20), ('w', 16), ('w', 16), ('w', 18), ('w', 18), ('w', 19), ('w', 19), ('w', 21),
+    ('w', 21), ('w', 19), ('w', 19), ('w', 17), ('w', 17), ('w', 20), ('w', 20), ('w', 20),
+    ('w', 20), ('w', 17), ('w', 17), ('w', 18), ('w', 18), ('w', 16), ('w', 16), ('w', 19),
+    ('w', 19), ('w', 21), ('w', 21), ('w', 21), ('w', 21), ('w', 18), ('w', 18), ('w', 20),
+    ('w', 20), ('w', 17), ('w', 17), ('w', 18), ('w', 18), ('w', 19), ('w', 19), ('w', 16),
+    ('w', 16), ('w', 21), ('w', 21), ('w', 20), ('w', 20), ('w', 17), ('w', 17), ('w', 16),
+    ('w', 19), ('w', 20), ('w', 18), ('w', 18), ('w', 21), ('w', 21), ('w', 17), ('w', 21),
+    ('w', 18),
 )
 
 
@@ -421,8 +245,9 @@
     return value.astype(jnp.float32)
 
 
-def reduce_steps(order, table, first_lane, given, theirs, landing, result, place, copies):
+def reduce_steps(order, table, first_lane, part_of, given, theirs, landing, result, place, copies):
     here = {"x": place.x, "y": place.y, "z": place.z}
+    every = pl.ds(0, 2) if part_of is None else pl.ds(part_of, 1)
 
     def region(done, where, half):
         def pick(axis, extent):
@@ -432,7 +257,13 @@
         if "z" in done:
             zl = pl.ds(lax.rem(where["z"], 2), 1)
             lanes = pl.ds(pl.multiple_of(first_lane + 128 * lax.div(where["z"], 2), 128), 128)
-        return table.at[pick("y", 4), zl, pick("x", 4), half, :, :, lanes]
+        if half is None:
+            rows = every, pl.ds(0, 2)
+        elif part_of is None:
+            rows = pl.ds(half, 1), pl.ds(0, 2)
+        else:
+            rows = every, pl.ds(half, 1)
+        return table.at[pick("y", 4), zl, pick("x", 4), *rows, :, lanes]
 
     partner_slot = copies.slot()
     copies.send(partner_slot, given, place.partner(), dst=theirs)
@@ -440,8 +271,8 @@
     copies.wait_recv(partner_slot, theirs, place.partner())
 
     def add_partner(y, carry):
-        at = (y, slice(None), slice(None), slice(None), slice(None), slice(None), pl.ds(first_lane, 256))
-        table[at] = (wide(table[at]) + wide(theirs[y])).astype(jnp.bfloat16)
+        own = table.at[y, :, :, every, :, :, pl.ds(first_lane, 256)]
+        own[...] = (wide(own[...]) + wide(theirs[y])).astype(jnp.bfloat16)
         return carry
 
     lax.fori_loop(0, 4, add_partner, 0)
@@ -451,6 +282,20 @@
         done = done + (axis,)
         at = {s: dict(here, **{axis: lax.rem(here[axis] + s + 4, 4)}) for s in (-1, 0, 1, 2)}
         ahead, behind = place.move(axis, 1), place.move(axis, -1)
+        if stage == 2:
+            slots = [copies.slot() for _ in range(3)]
+            for slot, step in enumerate((-1, 1, 2)):
+                copies.send(
+                    slots[slot], region(done, at[step], None), place.move(axis, step), dst=land.at[slot]
+                )
+            total = wide(region(done, at[0], None)[...])
+            for slot, step in enumerate((1, -1, 2)):
+                yield
+                copies.wait_recv(slots[slot], land.at[slot], place.move(axis, step))
+            total = total + wide(land[0]) + wide(land[1]) + wide(land[2])
+            count = 64 if part_of is None else 32
+            result[pl.ds(0 if part_of is None else 32 * part_of, count), :] = total.reshape(count, 128)
+            return
         slots = [copies.slot() for _ in range(6)]
 
         def send(slot, step, half, peer):
@@ -478,17 +323,16 @@
         for half in (0, 1):
             part = region(done, at[0], half)
             total = wide(part[...]) + wide(land[2 + half]) + wide(land[4 + half])
-            if stage == 2:
-                result[pl.ds(32 * half, 32), :] = total.reshape(32, 128)
-            else:
-                part[...] = total.astype(jnp.bfloat16)
-
-
-def stage_shape(order, stage):
+            part[...] = total.astype(jnp.bfloat16)
+
+
+def stage_shape(unit, part_of, order, stage):
     done = order[: stage + 1]
     x, y = (1 if axis in done else 4 for axis in "xy")
     zl, lanes = (1, 128) if "z" in done else (2, 256)
-    return (6, y, zl, x, 2, 16, lanes)
+    if stage == 2:
+        return (3, y, zl, x, 2 if part_of is None else 1, 2, 16, lanes)
+    return (6, y, zl, x, 1, 2 if part_of is None else 1, 16, lanes)
 
 
 def wrap32(value):
@@ -536,8 +380,9 @@
     qkv, out, normed, normed_t, signs, tangent, query, key, value, weights, context, context_t,
     tangent_context, part, cotangent, back_value, theirs, *rest,
 ):
-    landing, (send_sems, recv_sems, load_sems) = rest[:15], rest[15:]
+    landing, (send_sems, recv_sems, load_sems) = rest[:-3], rest[-3:]
     place = Place()
+    greet(place)
     bf16 = jnp.bfloat16
     loads = []
 
@@ -552,6 +397,7 @@
     def rows(w, columns):
         return w.at[place.c, :, :, columns]
 
+    load(hidden, normed)
     for h in range(4):
         load(rows(wq, pl.ds(h * 512, 512)), own(qkv.at[h], pl.ds(0, 512)))
         load(rows(wk, pl.ds(h * 128, 128)), own(qkv.at[h], pl.ds(512, 128)))
@@ -559,12 +405,13 @@
     for j in range(4):
         for p in range(4):
             load(rows(wo, pl.ds(512 * p + 128 * j, 128)), own(out.at[j], pl.ds(128 * p, 128)))
-    load(hidden, normed)
-    meet(place)
-    for copy in loads:
-        copy.wait()
     copies = Copies(send_sems, recv_sems)
     seed = seed_ref[0]
+
+    def enter():
+        for copy in loads:
+            copy.wait()
+        meet(place)
 
     def norm(i):
         at = pl.ds(128 * i, 128)
@@ -619,25 +466,34 @@
             context_t[head, at] = mixed[:, :128].T
 
     def probe(j):
-        for block in range(2):
-            at = pl.ds(256 * block, 256)
+        def one(block, carry):
+            at = pl.ds(pl.multiple_of(256 * block, 256), 256)
             part[j, :, at] = (dot(context[...], signs[j, :, at]) * 2048**-0.5).astype(bf16)
+            return carry
+
+        lax.fori_loop(0, 2, one, 0)
 
     def forward(j):
-        for block in range(2):
-            at = pl.ds(256 * block, 256)
+        def one(block, carry):
+            at = pl.ds(pl.multiple_of(256 * block, 256), 256)
             table = out[j, :, :, :, :, :, :, at].reshape(2048, 256)
-            total = (dot(tangent_context[...], table) + part[j, :, at].astype(jnp.float32)).astype(bf16)
-            cotangent[:, pl.ds(512 * j + 256 * block, 256)] = total
+            total = dot(tangent_context[...], table) + part[j, :, at].astype(jnp.float32)
+            cotangent[:, pl.ds(pl.multiple_of(512 * j + 256 * block, 256), 256)] = total.astype(bf16)
+            return carry
+
+        lax.fori_loop(0, 2, one, 0)
 
     def back(h):
-        table = jnp.concatenate([out[j, h].reshape(512, 512) for j in range(4)], 1)
-        for s in range(2):
-            at = pl.ds(SEQ * s, SEQ)
+        def one(s, carry):
+            table = jnp.concatenate([out[j, h].reshape(512, 512) for j in range(4)], 1)
+            at = pl.ds(pl.multiple_of(SEQ * s, SEQ), SEQ)
             turned = dot_t(table, cotangent[at, :]).astype(bf16)
             wide_row = jnp.concatenate([turned[128 * g : 128 * g + 128] for g in range(4)], 1)
             spread = dot(wide_row, weights[h, s].reshape(1024, SEQ)).astype(bf16)
             back_value[at, pl.ds(128 * h, 128)] = spread.T
+            return carry
+
+        lax.fori_loop(0, 2, one, 0)
 
     def own_term(unit, zh, core):
         side = lax.rem(place.c + core, 2)
@@ -667,32 +523,37 @@
 
         lax.fori_loop(0, 4, one, 0)
 
-    def reduce_walk(unit):
+    def reduce_walk(which):
+        unit, part_of, order = REDUCE_WALKS[which]
         mine = (0, 512) if unit == 4 else (unit, 0)
-        given = qkv.at[1, :, :, :, :, :, :, pl.ds(512, 256)]
-        if unit < 4:
-            given = qkv.at[unit, :, :, :, :, :, :, pl.ds(256, 256)]
+        every = pl.ds(0, 2) if part_of is None else pl.ds(part_of, 1)
+        source = (1, 512) if unit == 4 else (unit, 256)
         return reduce_steps(
-            REDUCE_ORDERS[unit],
+            order,
             qkv.at[mine[0]],
             mine[1],
-            given,
-            theirs.at[unit],
-            landing[3 * unit : 3 * unit + 3],
+            part_of,
+            qkv.at[source[0], :, :, :, every, :, :, pl.ds(source[1], 256)],
+            theirs.at[unit, :, :, :, every],
+            landing[3 * which : 3 * which + 3],
             value_ref if unit == 4 else out_ref.at[:, pl.ds(128 * unit, 128)],
             place,
             copies,
         )
 
-    walks = [gather_steps(qkv.at[h], GATHER_ORDERS[h], place, copies) for h in range(4)]
-    walks += [gather_steps(out.at[j], GATHER_ORDERS[4 + j], place, copies) for j in range(4)]
-    walks += [reduce_walk(unit) for unit in range(5)]
+    def gather_walk(chunk, first, columns, order):
+        buf = qkv.at[chunk] if chunk < 4 else out.at[chunk - 4]
+        return gather_steps(buf, pl.ds(first, columns), order, place, copies)
+
+    gathers = len(GATHER_WALKS)
+    walks = [gather_walk(*walk) for walk in GATHER_WALKS]
+    walks += [reduce_walk(which) for which in range(len(REDUCE_WALKS))]
     tasks = dict(
-        n=norm, t=tangents, s=sign_part, q=project, a=attend, p=probe, f=forward, b=back, m=terms
+        n=norm, t=tangents, s=sign_part, q=project, a=attend, p=probe, f=forward, b=back, m=terms, e=enter
     )
     for what, *where in SCHEDULE:
         if what == "w":
-            copies.early = where[0] < 4
+            copies.early = where[0] < gathers and GATHER_WALKS[where[0]][0] < 4
             next(walks[where[0]], None)
         else:
             tasks[what](*where)
@@ -705,7 +566,7 @@
 def whole(seed, hidden, gain, turns, wq, wk, wv, wo):
     bf16 = jnp.bfloat16
     halves = [w.reshape(2, 2, 16, w.shape[1]) for w in (wq, wk, wv, wo)]
-    copies = 210
+    copies = COPIES
     anywhere = pl.BlockSpec(memory_space=pl.ANY)
     vmem = pl.BlockSpec(memory_space=pltpu.VMEM)
     scratch = [
@@ -723,7 +584,7 @@
         (2048, 512),
         (512, 2048),
     ]
-    landings = [stage_shape(REDUCE_ORDERS[u], stage) for u in range(5) for stage in range(3)]
+    landings = [stage_shape(*walk, stage) for walk in REDUCE_WALKS for stage in range(3)]
     scratch += [(4, 512, 512), (512, 2048), (512, 512), (5, 4, 2, 4, 2, 2, 16, 256)] + landings
     return pl.pallas_call(
         whole_kernel,

time: 143 us -> 133 us (0.930)
  Pallas kernels: 138 us -> 128 us
    pallas_call x1, Pallas kernels: 138 us -> 128 us  [whole(): pl.pallas_call(whole_kernel, out_shape=[jax.ShapeDtypeStruct((64, 128), j...]
where the time goes in v4:
time: 133 us; the launch traced here: 132 us
  Pallas kernels  128 us (96%)
  local copies, waits for them, and re-layouts  2.94 us (2%)
    pallas_call x1, Pallas kernels, whole(): pl.pallas_call(whole_kernel, out_shape=[jax.ShapeDtypeStruct((64, 128), j...  128 us
    unnamed x2, local copies, waits for them, and re-layouts  2.94 us

profile of v4, /device:TPU:0, one launch (start us, length us, event | category | flops | bytes accessed | tf_op | source)
XLA Modules:
  0.0 132.4 jit_solution(16357097177341009002)
XLA Ops:
  1.3 128.2 %shard_map.95 = (f32[64,128]{1,0:T(8,128)}, f32[64,512]{1,0:T(8,128)}) custom-call(s32[1]{0:T(128)S(6)} %copy.12.seed_ref, bf16[2048]{0:T(1024)(128)(2,1)} %gain.1, f32[2,256,128]{2,1,0:T(8,128)} %constant.2.clone.turns, bf16[512,2048]{1,0:T(8,128)(2,1)} %hidden.1, bf16[2,2,16,2048]{3,2,1,0:T(8,128)(2,1)} %bitcast.4, bf16[2,2,16,512]{3,2,1,0:T(8,128)(2,1)} %bitcast.6, ...), custom_call_target="tpu_custom_call" | custom-call | tf_op jit(solution)/shard_map/pallas_call | solution.py:589
  129.5 1.4 %copy.13 = f32[64,128]{1,0:T(8,128)} copy(f32[64,128]{1,0:T(8,128)} %get-tuple-element.4) | data formatting | bytes 65536
  130.8 1.6 %copy.14 = f32[64,512]{1,0:T(8,128)} copy(f32[64,512]{1,0:T(8,128)} %get-tuple-element.5) | data formatting | bytes 262144

commit v5 on v4

v5 whole, which is shorter than its diff:
```python
import jax
import jax.numpy as jnp
import numpy as np
from jax import lax
from jax.experimental import pallas as pl
from jax.experimental.pallas import tpu as pltpu
from jax.sharding import PartitionSpec as P

MESH = pl.DeviceIdType.MESH
HEAD_DIM = 128
SEQ = 256
norm_eps = 1e-05
rope_base = 500000.0


class Place:
    def __init__(self):
        p = lax.axis_index("probe")
        f = lax.axis_index("fsdp")
        self.p, self.f = p, f
        self.x = lax.rem(f, 4)
        self.zl = lax.rem(lax.div(f, 4), 2)
        self.y = lax.div(f, 8)
        self.zh = lax.div(p, 2)
        self.c = lax.rem(p, 2)
        self.z = self.zh * 2 + self.zl

    def move(self, axis, step):
        x, y, z = self.x, self.y, self.z
        if axis == "x":
            x = lax.rem(x + step + 4, 4)
        elif axis == "y":
            y = lax.rem(y + step + 4, 4)
        else:
            z = lax.rem(z + step + 4, 4)
        return (lax.div(z, 2) * 2 + self.c, y * 8 + lax.rem(z, 2) * 4 + x)

    def partner(self):
        return (self.zh * 2 + 1 - self.c, self.f)

    def neighbours(self):
        return [self.move(a, s) for a in ("x", "y", "z") for s in (1, -1, 2)] + [self.partner()]


def greet(place):
    barrier = pltpu.get_barrier_semaphore()
    for peer in place.neighbours():
        pl.semaphore_signal(barrier, inc=1, device_id=peer, device_id_type=MESH)


def meet(place):
    pl.semaphore_wait(pltpu.get_barrier_semaphore(), len(place.neighbours()))


class Copies:
    def __init__(self, send_sems, recv_sems):
        self.send_sems, self.recv_sems = send_sems, recv_sems
        self.used = 0
        self.early = False
        self.started = []
        self.busy = [None] * SENDS

    def slot(self):
        self.used += 1
        return self.used - 1

    def send(self, slot, ref, peer, dst=None):
        at = len(self.started) % SENDS
        self.release(at)
        copy = pltpu.make_async_remote_copy(
            src_ref=ref,
            dst_ref=ref if dst is None else dst,
            send_sem=self.send_sems.at[at],
            recv_sem=self.recv_sems.at[slot],
            device_id=peer,
            device_id_type=MESH,
        )
        copy.start()
        self.started.append(copy)
        self.busy[at] = (self.early, copy)

    def release(self, at):
        if self.busy[at] is not None:
            self.busy[at][1].wait_send()
            self.busy[at] = None

    def wait_recv(self, slot, ref, peer):
        pltpu.make_async_remote_copy(
            src_ref=ref,
            dst_ref=ref,
            send_sem=self.send_sems.at[0],
            recv_sem=self.recv_sems.at[slot],
            device_id=peer,
            device_id_type=MESH,
        ).wait_recv()

    def finish(self, early_only=False):
        for at in range(SENDS):
            if self.busy[at] is not None and (self.busy[at][0] or not early_only):
                self.release(at)


def gather_steps(buf, lanes, order, place, copies):
    def region(have, where, core, halves, extra=()):
        def pick(axis, extent):
            if axis in extra:
                return pl.ds(0, 3)
            return pl.ds(0, extent) if axis in have else pl.ds(where[axis], 1)

        return buf.at[pick("y", 4), pick("z", 2), pick("x", 4), core, halves, :, lanes]

    here = {"x": place.x, "y": place.y, "z": place.zl}
    core, other, both = place.c, 1 - place.c, pl.ds(0, 2)
    partner = place.partner()
    partner_slot = copies.slot()

    def share(have, where):
        copies.send(partner_slot, region(have, where, core, both), partner)

    have = ()
    for phase, axis in enumerate(order):
        last = phase == 2
        if last:
            share(have, here)
        if axis == "z":
            slot = copies.slot()
            for half, step in ((0, 1), (1, -1)):
                copies.send(slot, region(have, here, core, pl.ds(half, 1)), place.move("z", step))
            there = dict(here, z=1 - place.zl)
            yield
            copies.wait_recv(slot, region(have, there, core, both), place.move("z", 1))
            if last:
                share(have, there)
        elif phase == 0:
            slot = copies.slot()
            for step in (-1, 1, 2):
                copies.send(slot, region(have, here, core, both), place.move(axis, step))
            yield
            copies.wait_recv(slot, region(have, here, core, both, (axis,)), place.move(axis, 1))
        else:
            at = {s: dict(here, **{axis: lax.rem(here[axis] + s + 4, 4)}) for s in (-1, 1, 2)}
            up, down, across = (copies.slot() for _ in range(3))
            ahead, behind = place.move(axis, 1), place.move(axis, -1)
            copies.send(up, region(have, here, core, both), ahead)
            copies.send(down, region(have, here, core, both), behind)
            yield
            copies.wait_recv(up, region(have, at[-1], core, both), behind)
            copies.send(across, region(have, at[-1], core, pl.ds(0, 1)), ahead)
            if last:
                share(have, at[-1])
            yield
            copies.wait_recv(down, region(have, at[1], core, both), ahead)
            copies.send(across, region(have, at[1], core, pl.ds(1, 1)), behind)
            if last:
                share(have, at[1])
            yield
            copies.wait_recv(across, region(have, at[2], core, both), behind)
            if last:
                share(have, at[2])
        have = have + (axis,)
    yield
    copies.wait_recv(partner_slot, region("xyz", here, other, both), partner)


GATHER_WALKS = (
    (0, 0, 256, ('z', 'x', 'y')),
    (0, 256, 256, ('y', 'x', 'z')),
    (0, 512, 256, ('x', 'y', 'z')),
    (1, 0, 256, ('y', 'x', 'z')),
    (1, 256, 256, ('z', 'y', 'x')),
    (1, 512, 256, ('x', 'y', 'z')),
    (2, 0, 256, ('y', 'z', 'x')),
    (2, 256, 256, ('y', 'x', 'z')),
    (2, 512, 256, ('y', 'x', 'z')),
    (3, 0, 256, ('z', 'y', 'x')),
    (3, 256, 256, ('z', 'x', 'y')),
    (3, 512, 256, ('x', 'z', 'y')),
    (4, 0, 512, ('y', 'x', 'z')),
    (5, 0, 512, ('y', 'z', 'x')),
    (6, 0, 512, ('x', 'y', 'z')),
    (7, 0, 512, ('x', 'z', 'y')),
)
REDUCE_WALKS = (
    (0, None, ('z', 'y', 'x')),
    (1, None, ('z', 'x', 'y')),
    (2, None, ('x', 'z', 'y')),
    (3, None, ('y', 'x', 'z')),
    (4, 0, ('z', 'y', 'x')),
    (4, 1, ('y', 'x', 'z')),
)
SENDS = 64
RECEIVES = 168
SCHEDULE = (
    ('s', 2), ('s', 3), ('e',), ('w', 0), ('w', 1), ('w', 2), ('w', 3), ('w', 4), ('w', 5),
    ('w', 6), ('w', 7), ('w', 8), ('w', 9), ('w', 10), ('w', 11), ('n', 0), ('n', 1), ('w', 0),
    ('n', 2), ('n', 3), ('w', 4), ('t', 0), ('w', 1), ('w', 2), ('w', 3), ('w', 5), ('w', 9),
    ('w', 10), ('t', 1), ('w', 0), ('w', 0), ('w', 4), ('w', 4), ('w', 6), ('w', 7), ('w', 8),
    ('w', 11), ('w', 1), ('w', 1), ('s', 0), ('w', 2), ('w', 2), ('w', 3), ('w', 3), ('s', 1),
    ('w', 0), ('w', 5), ('w', 5), ('w', 6), ('w', 10), ('w', 10), ('w', 11), ('w', 9), ('w', 9),
    ('w', 4), ('s', 4), ('w', 2), ('w', 7), ('w', 7), ('s', 5), ('w', 8), ('w', 8), ('s', 6),
    ('w', 1), ('w', 3), ('w', 0), ('w', 0), ('s', 7), ('w', 5), ('w', 2), ('w', 6), ('w', 6),
    ('w', 10), ('w', 11), ('w', 11), ('w', 9), ('w', 1), ('w', 2), ('w', 12), ('w', 0), ('w', 4),
    ('w', 4), ('w', 7), ('w', 8), ('w', 3), ('w', 1), ('w', 13), ('w', 10), ('w', 10), ('w', 0),
    ('w', 6), ('w', 14), ('q', 0), ('w', 5), ('w', 11), ('a', 0, 0), ('w', 3), ('w', 4), ('w', 6),
    ('w', 9), ('w', 9), ('w', 12), ('w', 15), ('a', 0, 1), ('w', 4), ('w', 5), ('w', 7), ('w', 10),
    ('w', 11), ('w', 13), ('w', 14), ('q', 1), ('w', 8), ('w', 9), ('w', 7), ('a', 1, 0), ('w', 10),
    ('w', 12), ('w', 12), ('w', 13), ('a', 1, 1), ('w', 8), ('w', 9), ('w', 14), ('w', 14),
    ('w', 15), ('q', 2), ('w', 12), ('a', 2, 0), ('w', 14), ('w', 15), ('a', 2, 1), ('q', 3),
    ('w', 13), ('w', 13), ('a', 3, 0), ('w', 12), ('a', 3, 1), ('w', 15), ('w', 15), ('p', 0),
    ('w', 13), ('p', 1), ('w', 12), ('f', 0), ('w', 14), ('m', 0), ('w', 16), ('w', 13), ('f', 1),
    ('w', 15), ('m', 1), ('w', 17), ('w', 14), ('p', 2), ('f', 2), ('m', 2), ('w', 18), ('w', 15),
    ('w', 16), ('p', 3), ('f', 3), ('w', 17), ('m', 3), ('w', 19), ('b', 0), ('w', 16), ('w', 16),
    ('w', 18), ('b', 1), ('w', 19), ('b', 2), ('w', 17), ('w', 17), ('w', 18), ('w', 18), ('b', 3),
    ('m', 4), ('w', 20), ('w', 21), ('w', 19), ('w', 19), ('w', 16), ('w', 18), ('w', 17),
    ('w', 20), ('w', 21), ('w', 18), ('w', 18), ('w', 19), ('w', 16), ('w', 16), ('w', 17),
    ('w', 17), ('w', 20), ('w', 20), ('w', 21), ('w', 21), ('w', 19), ('w', 19), ('w', 18),
    ('w', 17), ('w', 16), ('w', 20), ('w', 19), ('w', 21), ('w', 18), ('w', 20), ('w', 20),
    ('w', 21), ('w', 21), ('w', 16), ('w', 17), ('w', 19), ('w', 20), ('w', 21), ('w', 20),
    ('w', 21),
)


def wide(value):
    return value.astype(jnp.float32)


def reduce_steps(order, table, first_lane, part_of, given, theirs, landing, result, place, copies):
    here = {"x": place.x, "y": place.y, "z": place.z}
    every = pl.ds(0, 2) if part_of is None else pl.ds(part_of, 1)

    def region(done, where, half):
        def pick(axis, extent):
            return pl.ds(where[axis], 1) if axis in done else pl.ds(0, extent)

        zl, lanes = pl.ds(0, 2), pl.ds(first_lane, 256)
        if "z" in done:
            zl = pl.ds(lax.rem(where["z"], 2), 1)
            lanes = pl.ds(pl.multiple_of(first_lane + 128 * lax.div(where["z"], 2), 128), 128)
        if half is None:
            rows = every, pl.ds(0, 2)
        elif part_of is None:
            rows = pl.ds(half, 1), pl.ds(0, 2)
        else:
            rows = every, pl.ds(half, 1)
        return table.at[pick("y", 4), zl, pick("x", 4), *rows, :, lanes]

    partner_slot = copies.slot()
    copies.send(partner_slot, given, place.partner(), dst=theirs)
    yield
    copies.wait_recv(partner_slot, theirs, place.partner())

    def add_partner(y, carry):
        own = table.at[y, :, :, every, :, :, pl.ds(first_lane, 256)]
        own[...] = (wide(own[...]) + wide(theirs[y])).astype(jnp.bfloat16)
        return carry

    lax.fori_loop(0, 4, add_partner, 0)
    done = ()
    for stage, axis in enumerate(order):
        land = landing[stage]
        done = done + (axis,)
        at = {s: dict(here, **{axis: lax.rem(here[axis] + s + 4, 4)}) for s in (-1, 0, 1, 2)}
        ahead, behind = place.move(axis, 1), place.move(axis, -1)
        if stage == 2:
            slot = copies.slot()
            for n, step in enumerate((-1, 1, 2)):
                copies.send(slot, region(done, at[step], None), place.move(axis, step), dst=land.at[n])
            total = wide(region(done, at[0], None)[...])
            yield
            copies.wait_recv(slot, land, ahead)
            total = total + wide(land[0]) + wide(land[1]) + wide(land[2])
            count = 64 if part_of is None else 32
            result[pl.ds(0 if part_of is None else 32 * part_of, count), :] = total.reshape(count, 128)
            return
        first, second, rest = (copies.slot() for _ in range(3))

        def send(slot, step, half, peer, to):
            copies.send(slot, region(done, at[step], half), peer, dst=land.at[to])

        send(first, 2, 0, ahead, 0)
        send(second, 2, 1, behind, 1)
        send(rest, 1, 1, ahead, 3)
        send(rest, -1, 0, behind, 4)
        for slot, at_slot, step, half, source, peer, onward in (
            (first, 0, 1, 0, behind, ahead, 2),
            (second, 1, -1, 1, ahead, behind, 5),
        ):
            yield
            copies.wait_recv(slot, land.at[at_slot], source)
            part = region(done, at[step], half)
            part[...] = (wide(part[...]) + wide(land[at_slot])).astype(jnp.bfloat16)
            send(rest, step, half, peer, onward)
        yield
        copies.wait_recv(rest, land.at[pl.ds(2, 4)], behind)
        for half in (0, 1):
            part = region(done, at[0], half)
            total = wide(part[...]) + wide(land[2 + half]) + wide(land[4 + half])
            part[...] = total.astype(jnp.bfloat16)


def stage_shape(unit, part_of, order, stage):
    done = order[: stage + 1]
    x, y = (1 if axis in done else 4 for axis in "xy")
    zl, lanes = (1, 128) if "z" in done else (2, 256)
    if stage == 2:
        return (3, y, zl, x, 2 if part_of is None else 1, 2, 16, lanes)
    return (6, y, zl, x, 1, 2 if part_of is None else 1, 16, lanes)


def wrap32(value):
    value &= 0xFFFFFFFF
    return value - (1 << 32) if value >= 1 << 31 else value


MIX = 747796405


def fill_signs(dst, seed, code, table_columns, first_row, row_total, first_column, spread):
    width = dst.shape[1]
    step = 32
    lanes = lax.broadcasted_iota(jnp.int32, (step, width), 1)
    if spread:
        lanes = lanes + lax.div(lanes, 128) * 384
    tile = (lax.broadcasted_iota(jnp.int32, (step, width), 0) * table_columns + lanes) * MIX
    base = seed * 1664525 + wrap32(code * 374761393 + first_column * MIX)

    def one(i, carry):
        row = first_row + i * step
        hashed = tile + (base + row * wrap32(table_columns * MIX))
        hashed = hashed ^ lax.shift_right_logical(hashed, jnp.int32(15))
        hashed = hashed * 668265261
        hashed = hashed ^ lax.shift_right_logical(hashed, jnp.int32(13))
        hashed = hashed * 1274126177
        hashed = hashed ^ lax.shift_right_logical(hashed, jnp.int32(16))
        signs = jnp.where((hashed & 1) == 1, jnp.float32(1.0), jnp.float32(-1.0))
        dst[pl.ds(pl.multiple_of(row, step), step), :] = signs.astype(jnp.bfloat16)
        return carry

    lax.fori_loop(0, row_total // step, one, 0)


def dot(a, b):
    return jnp.dot(a, b, preferred_element_type=jnp.float32)


def dot_t(a, b):
    return lax.dot_general(a, b, (((1,), (1,)), ((), ())), preferred_element_type=jnp.float32)


def whole_kernel(
    seed_ref, gain, turns, hidden, wq, wk, wv, wo, value_ref, out_ref,
    qkv, out, normed, normed_t, signs, tangent, query, key, value, weights, context, context_t,
    tangent_context, part, cotangent, back_value, theirs, *rest,
):
    landing, (send_sems, recv_sems, load_sems) = rest[:-3], rest[-3:]
    place = Place()
    greet(place)
    bf16 = jnp.bfloat16

    def load(src, dst, sem):
        pltpu.make_async_copy(src, dst, load_sems.at[sem]).start()

    def own(buf, columns):
        return buf.at[place.y, place.zl, place.x, place.c, :, :, columns]

    def rows(w, columns):
        return w.at[place.c, :, :, columns]

    load(hidden, normed, 0)
    for h in range(4):
        load(rows(wq, pl.ds(h * 512, 512)), own(qkv.at[h], pl.ds(0, 512)), 1)
        load(rows(wk, pl.ds(h * 128, 128)), own(qkv.at[h], pl.ds(512, 128)), 1)
        load(rows(wv, pl.ds(h * 128, 128)), own(qkv.at[h], pl.ds(640, 128)), 1)
    for j in range(4):
        for p in range(4):
            load(rows(wo, pl.ds(512 * p + 128 * j, 128)), own(out.at[j], pl.ds(128 * p, 128)), 2)
    copies = Copies(send_sems, recv_sems)
    seed = seed_ref[0]

    def enter():
        pltpu.make_async_copy(hidden, normed, load_sems.at[0]).wait()
        for buf, sem in ((qkv, 1), (out, 2)):
            landed = buf.at[:, place.y, place.zl, place.x, place.c]
            pltpu.make_async_copy(landed, landed, load_sems.at[sem]).wait()
        meet(place)

    def norm(i):
        at = pl.ds(128 * i, 128)
        x = normed[at, :].astype(jnp.float32)
        inverse = lax.rsqrt(jnp.mean(x * x, axis=1, keepdims=True) + norm_eps)
        n = (x * inverse * gain[...][None, :].astype(jnp.float32)).astype(bf16)
        normed[at, :] = n
        normed_t[:, at] = n.T

    def tangents(i):
        table = signs.at[0, :, pl.ds(256 * i, 256)]
        fill_signs(table, seed, 0, 512, 0, 2048, 256 * i, False)
        tangent[:, pl.ds(256 * i, 256)] = (dot(normed[...], table[...]) * 2048**-0.5).astype(bf16)

    def sign_part(i):
        fill_signs(signs.at[i // 2], seed, 1, 2048, 1024 * (i % 2), 1024, 128 * (i // 2), True)

    def project(h):
        cosine = jnp.concatenate([turns[0], turns[0]], 0)
        sine = jnp.concatenate([turns[1], turns[1]], 0)

        def rope(x):
            return (x * cosine + pltpu.roll(x, 64, 1) * sine).astype(bf16)

        for block in range(3):
            table = qkv[h, :, :, :, :, :, :, pl.ds(256 * block, 256)].reshape(2048, 256)
            raw = dot(normed[...], table)
            left, right = raw[:, :128], raw[:, 128:]
            if block < 2:
                query[2 * block] = rope(left)
                query[2 * block + 1] = rope(right)
            else:
                key[...] = rope(left)
                value[:, pl.ds(0, 128)] = right.astype(bf16)
                value[:, pl.ds(128, 128)] = tangent[:, pl.ds(128 * h, 128)]

    def attend(h, pair):
        causal = lax.broadcasted_iota(jnp.int32, (SEQ, SEQ), 0) >= lax.broadcasted_iota(
            jnp.int32, (SEQ, SEQ), 1
        )

        def one(g, carry):
            head = pl.ds(pl.multiple_of(128 * (4 * h + g), 128), 128)
            for s in range(2):
                at = pl.ds(SEQ * s, SEQ)
                scores = dot_t(query[g, at, :], key[at, :]) * HEAD_DIM**-0.5
                scores = jnp.where(causal, scores, -1e30)
                raised = jnp.exp(scores - jnp.max(scores, axis=1, keepdims=True))
                chances = (raised * (1.0 / jnp.sum(raised, axis=1, keepdims=True))).astype(bf16)
                weights[h, s, g] = chances
                mixed = dot(chances, value[at, :]).astype(bf16)
                context[at, head] = mixed[:, :128]
                tangent_context[at, head] = mixed[:, 128:]
                context_t[head, at] = mixed[:, :128].T
            return carry

        lax.fori_loop(2 * pair, 2 * pair + 2, one, 0)

    def probe(j):
        for block in range(2):
            at = pl.ds(256 * block, 256)
            part[j, :, at] = (dot(context[...], signs[j, :, at]) * 2048**-0.5).astype(bf16)

    def forward(j):
        for block in range(2):
            at = pl.ds(256 * block, 256)
            table = out[j, :, :, :, :, :, :, at].reshape(2048, 256)
            total = dot(tangent_context[...], table) + part[j, :, at].astype(jnp.float32)
            cotangent[:, pl.ds(512 * j + 256 * block, 256)] = total.astype(bf16)

    def back(h):
        table = jnp.concatenate([out[j, h].reshape(512, 512) for j in range(4)], 1)
        for s in range(2):
            at = pl.ds(SEQ * s, SEQ)
            turned = dot_t(table, cotangent[at, :]).astype(bf16)
            wide_row = jnp.concatenate([turned[128 * g : 128 * g + 128] for g in range(4)], 1)
            spread = dot(wide_row, weights[h, s].reshape(1024, SEQ)).astype(bf16)
            back_value[at, pl.ds(128 * h, 128)] = spread.T

    def own_term(unit, zh, core):
        side = lax.rem(place.c + core, 2)
        if unit == 4:
            return side, pl.ds(512 + 128 * zh, 128)
        return unit, pl.ds(pl.multiple_of(256 * side + 128 * zh, 128), 128)

    def terms(unit):
        if unit == TERM_FIRST:
            copies.finish(early_only=True)
        left = normed_t if unit == 4 else context_t

        def one(trip, carry):
            for zh in range(2):
                if unit == 4:
                    right = back_value[:, pl.ds(256 * zh, 256)]
                else:
                    right = cotangent[:, pl.ds(512 * unit + 256 * zh, 256)]
                both = dot(left[pl.ds(pl.multiple_of(1024 * trip, 1024), 1024), :], right).astype(bf16)
                for core in range(2):
                    h, lanes = own_term(unit, zh, core)
                    qkv[h, pl.ds(2 * trip, 2), :, :, :, :, :, lanes] = both[
                        :, 128 * core : 128 * core + 128
                    ].reshape(2, 2, 4, 2, 2, 16, 128)
            return carry

        lax.fori_loop(0, 2, one, 0)

    def reduce_walk(which):
        unit, part_of, order = REDUCE_WALKS[which]
        mine = (0, 512) if unit == 4 else (unit, 0)
        every = pl.ds(0, 2) if part_of is None else pl.ds(part_of, 1)
        source = (1, 512) if unit == 4 else (unit, 256)
        return reduce_steps(
            order,
            qkv.at[mine[0]],
            mine[1],
            part_of,
            qkv.at[source[0], :, :, :, every, :, :, pl.ds(source[1], 256)],
            theirs.at[unit, :, :, :, every],
            landing[3 * which : 3 * which + 3],
            value_ref if unit == 4 else out_ref.at[:, pl.ds(128 * unit, 128)],
            place,
            copies,
        )

    def gather_walk(chunk, first, columns, order):
        buf = qkv.at[chunk] if chunk < 4 else out.at[chunk - 4]
        return gather_steps(buf, pl.ds(first, columns), order, place, copies)

    gathers = len(GATHER_WALKS)
    walks = [gather_walk(*walk) for walk in GATHER_WALKS]
    walks += [reduce_walk(which) for which in range(len(REDUCE_WALKS))]
    tasks = dict(
        n=norm, t=tangents, s=sign_part, q=project, a=attend, p=probe, f=forward, b=back, m=terms, e=enter
    )
    for what, *where in SCHEDULE:
        if what == "w":
            copies.early = where[0] < gathers and GATHER_WALKS[where[0]][0] < 4
            next(walks[where[0]], None)
        else:
            tasks[what](*where)
    copies.finish()


TERM_FIRST = [where[0] for what, *where in SCHEDULE if what == "m"][0]


def whole(seed, hidden, gain, turns, wq, wk, wv, wo):
    bf16 = jnp.bfloat16
    halves = [w.reshape(2, 2, 16, w.shape[1]) for w in (wq, wk, wv, wo)]
    anywhere = pl.BlockSpec(memory_space=pl.ANY)
    vmem = pl.BlockSpec(memory_space=pltpu.VMEM)
    scratch = [
        (4, 4, 2, 4, 2, 2, 16, 768),
        (4, 4, 2, 4, 2, 2, 16, 512),
        (512, 2048),
        (2048, 512),
        (4, 2048, 512),
        (512, 512),
        (4, 512, 128),
        (512, 128),
        (512, 256),
        (4, 2, 4, SEQ, SEQ),
        (512, 2048),
        (2048, 512),
        (512, 2048),
    ]
    landings = [stage_shape(*walk, stage) for walk in REDUCE_WALKS for stage in range(3)]
    scratch += [(4, 512, 512), (512, 2048), (512, 512), (5, 4, 2, 4, 2, 2, 16, 256)] + landings
    return pl.pallas_call(
        whole_kernel,
        out_shape=[
            jax.ShapeDtypeStruct((64, 128), jnp.float32),
            jax.ShapeDtypeStruct((64, 512), jnp.float32),
        ],
        in_specs=[pl.BlockSpec(memory_space=pltpu.SMEM)] + [vmem] * 2 + [anywhere] * 5,
        out_specs=[vmem] * 2,
        scratch_shapes=[pltpu.VMEM(s, bf16) for s in scratch]
        + [
            pltpu.SemaphoreType.DMA((SENDS,)),
            pltpu.SemaphoreType.DMA((RECEIVES,)),
            pltpu.SemaphoreType.DMA((3,)),
        ],
        compiler_params=pltpu.CompilerParams(
            collective_id=0, has_side_effects=True, vmem_limit_bytes=67043328
        ),
    )(seed, gain, turns, hidden, *halves)


def turn_tables():
    exponent = np.arange(64, dtype=np.float64) * (-2.0 / HEAD_DIM)
    angles = np.arange(SEQ, dtype=np.float64)[:, None] * np.power(rope_base, exponent)[None, :]
    cosine, sine = np.cos(angles), np.sin(angles)
    return np.stack(
        [np.concatenate([cosine, cosine], 1), np.concatenate([-sine, sine], 1)]
    ).astype(np.float32)

def body(hidden, norm_gain, query_weight, key_weight, value_weight, output_weight, probe_seed):
    return tuple(
        whole(
            probe_seed,
            hidden,
            norm_gain,
            jnp.asarray(turn_tables()),
            query_weight,
            key_weight,
            value_weight,
            output_weight,
        )
    )


def solution(mesh):
    return jax.shard_map(
        body,
        mesh=mesh,
        in_specs=(
            P(("probe", "fsdp"), None),
            P(),
            P("fsdp", None),
            P("fsdp", None),
            P("fsdp", None),
            P("fsdp", None),
            P("probe"),
        ),
        out_specs=(P("fsdp", "probe"), P("fsdp", "probe")),
        check_vma=False,
    )
```

time: 133 us -> 117 us (0.88)
  Pallas kernels: 128 us -> 113 us
    pallas_call x1, Pallas kernels: 128 us -> 113 us  [whole(): pl.pallas_call(whole_kernel, out_shape=[jax.ShapeDtypeStruct((64, 128), j...]
where the time goes in v5:
time: 117 us
  Pallas kernels  113 us (97%)
  local copies, waits for them, and re-layouts  2.94 us (3%)
  between operations  1.29 us (1%)
    pallas_call x1, Pallas kernels, whole(): pl.pallas_call(whole_kernel, out_shape=[jax.ShapeDtypeStruct((64, 128), j...  113 us
    unnamed x2, local copies, waits for them, and re-layouts  2.94 us

profile of v5, /device:TPU:0, one launch (start us, length us, event | category | flops | bytes accessed | tf_op | source)
XLA Modules:
  0.0 117.2 jit_solution(7574862378979541681)
XLA Ops:
  1.3 113.0 %shard_map.95 = (f32[64,128]{1,0:T(8,128)}, f32[64,512]{1,0:T(8,128)}) custom-call(s32[1]{0:T(128)S(6)} %copy.12.seed_ref, bf16[2048]{0:T(1024)(128)(2,1)} %gain.1, f32[2,256,128]{2,1,0:T(8,128)} %constant.2.clone.turns, bf16[512,2048]{1,0:T(8,128)(2,1)} %hidden.1, bf16[2,2,16,2048]{3,2,1,0:T(8,128)(2,1)} %bitcast.4, bf16[2,2,16,512]{3,2,1,0:T(8,128)(2,1)} %bitcast.6, ...), custom_call_target="tpu_custom_call" | custom-call | tf_op jit(solution)/shard_map/pallas_call | solution.py:554
  114.3 1.4 %copy.13 = f32[64,128]{1,0:T(8,128)} copy(f32[64,128]{1,0:T(8,128)} %get-tuple-element.4) | data formatting | bytes 65536
  115.7 1.6 %copy.14 = f32[64,512]{1,0:T(8,128)} copy(f32[64,512]{1,0:T(8,128)} %get-tuple-element.5) | data formatting | bytes 262144

commit v6 on v5

--- a/solution.py
+++ b/solution.py
@@ -163,60 +163,59 @@
 
 
 GATHER_WALKS = (
-    (0, 0, 256, ('z', 'x', 'y')),
+    (0, 0, 256, ('x', 'y', 'z')),
     (0, 256, 256, ('y', 'x', 'z')),
-    (0, 512, 256, ('x', 'y', 'z')),
-    (1, 0, 256, ('y', 'x', 'z')),
-    (1, 256, 256, ('z', 'y', 'x')),
-    (1, 512, 256, ('x', 'y', 'z')),
+    (0, 512, 256, ('y', 'z', 'x')),
+    (1, 0, 256, ('x', 'z', 'y')),
+    (1, 256, 256, ('x', 'y', 'z')),
+    (1, 512, 256, ('y', 'x', 'z')),
     (2, 0, 256, ('y', 'z', 'x')),
-    (2, 256, 256, ('y', 'x', 'z')),
-    (2, 512, 256, ('y', 'x', 'z')),
+    (2, 256, 256, ('x', 'y', 'z')),
+    (2, 512, 256, ('x', 'z', 'y')),
     (3, 0, 256, ('z', 'y', 'x')),
-    (3, 256, 256, ('z', 'x', 'y')),
-    (3, 512, 256, ('x', 'z', 'y')),
-    (4, 0, 512, ('y', 'x', 'z')),
-    (5, 0, 512, ('y', 'z', 'x')),
-    (6, 0, 512, ('x', 'y', 'z')),
+    (3, 256, 256, ('x', 'y', 'z')),
+    (3, 512, 256, ('x', 'y', 'z')),
+    (4, 0, 512, ('x', 'y', 'z')),
+    (5, 0, 512, ('z', 'y', 'x')),
+    (6, 0, 512, ('y', 'x', 'z')),
     (7, 0, 512, ('x', 'z', 'y')),
 )
 REDUCE_WALKS = (
-    (0, None, ('z', 'y', 'x')),
-    (1, None, ('z', 'x', 'y')),
-    (2, None, ('x', 'z', 'y')),
-    (3, None, ('y', 'x', 'z')),
-    (4, 0, ('z', 'y', 'x')),
-    (4, 1, ('y', 'x', 'z')),
+    (0, None, ('x', 'z', 'y')),
+    (1, None, ('x', 'y', 'z')),
+    (2, None, ('y', 'x', 'z')),
+    (3, None, ('z', 'x', 'y')),
+    (4, 0, ('x', 'z', 'y')),
+    (4, 1, ('z', 'x', 'y')),
 )
 SENDS = 64
-RECEIVES = 168
+RECEIVES = 164
 SCHEDULE = (
     ('s', 2), ('s', 3), ('e',), ('w', 0), ('w', 1), ('w', 2), ('w', 3), ('w', 4), ('w', 5),
-    ('w', 6), ('w', 7), ('w', 8), ('w', 9), ('w', 10), ('w', 11), ('n', 0), ('n', 1), ('w', 0),
-    ('n', 2), ('n', 3), ('w', 4), ('t', 0), ('w', 1), ('w', 2), ('w', 3), ('w', 5), ('w', 9),
-    ('w', 10), ('t', 1), ('w', 0), ('w', 0), ('w', 4), ('w', 4), ('w', 6), ('w', 7), ('w', 8),
-    ('w', 11), ('w', 1), ('w', 1), ('s', 0), ('w', 2), ('w', 2), ('w', 3), ('w', 3), ('s', 1),
-    ('w', 0), ('w', 5), ('w', 5), ('w', 6), ('w', 10), ('w', 10), ('w', 11), ('w', 9), ('w', 9),
-    ('w', 4), ('s', 4), ('w', 2), ('w', 7), ('w', 7), ('s', 5), ('w', 8), ('w', 8), ('s', 6),
-    ('w', 1), ('w', 3), ('w', 0), ('w', 0), ('s', 7), ('w', 5), ('w', 2), ('w', 6), ('w', 6),
-    ('w', 10), ('w', 11), ('w', 11), ('w', 9), ('w', 1), ('w', 2), ('w', 12), ('w', 0), ('w', 4),
-    ('w', 4), ('w', 7), ('w', 8), ('w', 3), ('w', 1), ('w', 13), ('w', 10), ('w', 10), ('w', 0),
-    ('w', 6), ('w', 14), ('q', 0), ('w', 5), ('w', 11), ('a', 0, 0), ('w', 3), ('w', 4), ('w', 6),
-    ('w', 9), ('w', 9), ('w', 12), ('w', 15), ('a', 0, 1), ('w', 4), ('w', 5), ('w', 7), ('w', 10),
-    ('w', 11), ('w', 13), ('w', 14), ('q', 1), ('w', 8), ('w', 9), ('w', 7), ('a', 1, 0), ('w', 10),
-    ('w', 12), ('w', 12), ('w', 13), ('a', 1, 1), ('w', 8), ('w', 9), ('w', 14), ('w', 14),
-    ('w', 15), ('q', 2), ('w', 12), ('a', 2, 0), ('w', 14), ('w', 15), ('a', 2, 1), ('q', 3),
-    ('w', 13), ('w', 13), ('a', 3, 0), ('w', 12), ('a', 3, 1), ('w', 15), ('w', 15), ('p', 0),
-    ('w', 13), ('p', 1), ('w', 12), ('f', 0), ('w', 14), ('m', 0), ('w', 16), ('w', 13), ('f', 1),
-    ('w', 15), ('m', 1), ('w', 17), ('w', 14), ('p', 2), ('f', 2), ('m', 2), ('w', 18), ('w', 15),
-    ('w', 16), ('p', 3), ('f', 3), ('w', 17), ('m', 3), ('w', 19), ('b', 0), ('w', 16), ('w', 16),
-    ('w', 18), ('b', 1), ('w', 19), ('b', 2), ('w', 17), ('w', 17), ('w', 18), ('w', 18), ('b', 3),
-    ('m', 4), ('w', 20), ('w', 21), ('w', 19), ('w', 19), ('w', 16), ('w', 18), ('w', 17),
-    ('w', 20), ('w', 21), ('w', 18), ('w', 18), ('w', 19), ('w', 16), ('w', 16), ('w', 17),
-    ('w', 17), ('w', 20), ('w', 20), ('w', 21), ('w', 21), ('w', 19), ('w', 19), ('w', 18),
-    ('w', 17), ('w', 16), ('w', 20), ('w', 19), ('w', 21), ('w', 18), ('w', 20), ('w', 20),
-    ('w', 21), ('w', 21), ('w', 16), ('w', 17), ('w', 19), ('w', 20), ('w', 21), ('w', 20),
-    ('w', 21),
+    ('w', 6), ('w', 7), ('w', 8), ('w', 9), ('w', 10), ('w', 11), ('n', 1), ('n', 2), ('n', 0),
+    ('n', 3), ('t', 0), ('w', 0), ('w', 1), ('w', 2), ('w', 3), ('w', 9), ('t', 1), ('w', 4),
+    ('w', 5), ('w', 6), ('w', 7), ('w', 8), ('w', 2), ('w', 0), ('w', 0), ('s', 0), ('w', 3),
+    ('w', 9), ('w', 9), ('w', 10), ('s', 5), ('w', 1), ('w', 1), ('w', 4), ('w', 4), ('w', 6),
+    ('w', 8), ('w', 11), ('s', 4), ('w', 5), ('w', 5), ('w', 7), ('w', 7), ('s', 7), ('w', 0),
+    ('s', 1), ('w', 2), ('w', 2), ('s', 6), ('w', 1), ('w', 3), ('w', 3), ('w', 9), ('w', 10),
+    ('w', 10), ('w', 6), ('w', 6), ('w', 4), ('w', 0), ('w', 5), ('w', 2), ('w', 8), ('w', 8),
+    ('w', 1), ('w', 0), ('w', 12), ('w', 11), ('w', 11), ('w', 2), ('w', 13), ('w', 9), ('w', 9),
+    ('w', 7), ('w', 1), ('w', 14), ('w', 4), ('q', 0), ('w', 3), ('w', 6), ('w', 10), ('a', 0, 0),
+    ('w', 4), ('w', 5), ('w', 8), ('w', 9), ('w', 11), ('w', 12), ('w', 13), ('w', 15), ('w', 3),
+    ('a', 0, 1), ('w', 6), ('w', 14), ('w', 7), ('w', 5), ('q', 1), ('w', 8), ('w', 9), ('a', 1, 0),
+    ('w', 7), ('w', 10), ('w', 12), ('w', 12), ('w', 15), ('a', 1, 1), ('w', 13), ('w', 13),
+    ('w', 14), ('w', 14), ('q', 2), ('w', 10), ('w', 11), ('w', 12), ('w', 15), ('a', 2, 1),
+    ('w', 13), ('w', 14), ('a', 2, 0), ('w', 11), ('q', 3), ('a', 3, 0), ('a', 3, 1), ('w', 12),
+    ('w', 15), ('w', 15), ('p', 3), ('w', 13), ('w', 13), ('p', 1), ('p', 2), ('w', 12), ('p', 0),
+    ('w', 15), ('f', 0), ('w', 13), ('w', 14), ('m', 0), ('w', 16), ('w', 15), ('f', 3), ('m', 3),
+    ('w', 19), ('w', 13), ('w', 14), ('f', 1), ('m', 1), ('w', 17), ('f', 2), ('w', 16), ('b', 2),
+    ('w', 19), ('w', 17), ('b', 3), ('w', 16), ('w', 16), ('m', 2), ('w', 18), ('b', 1), ('w', 19),
+    ('w', 19), ('b', 0), ('w', 17), ('w', 17), ('w', 18), ('m', 4), ('w', 20), ('w', 21), ('w', 19),
+    ('w', 16), ('w', 20), ('w', 18), ('w', 18), ('w', 21), ('w', 16), ('w', 16), ('w', 17),
+    ('w', 19), ('w', 19), ('w', 20), ('w', 20), ('w', 21), ('w', 21), ('w', 18), ('w', 19),
+    ('w', 17), ('w', 17), ('w', 16), ('w', 20), ('w', 21), ('w', 18), ('w', 18), ('w', 20),
+    ('w', 20), ('w', 17), ('w', 19), ('w', 21), ('w', 21), ('w', 18), ('w', 16), ('w', 20),
+    ('w', 21), ('w', 17), ('w', 20), ('w', 18), ('w', 21),
 )
 
 
@@ -348,7 +347,7 @@
 
 
 def whole_kernel(
-    seed_ref, gain, turns, hidden, wq, wk, wv, wo, value_ref, out_ref,
+    seed_ref, gain, turns, hidden, wq, wk, wv, wo, result,
     qkv, out, normed, normed_t, signs, tangent, query, key, value, weights, context, context_t,
     tangent_context, part, cotangent, back_value, theirs, *rest,
 ):
@@ -454,13 +453,16 @@
             cotangent[:, pl.ds(512 * j + 256 * block, 256)] = total.astype(bf16)
 
     def back(h):
-        table = jnp.concatenate([out[j, h].reshape(512, 512) for j in range(4)], 1)
-        for s in range(2):
-            at = pl.ds(SEQ * s, SEQ)
+        def one(s, carry):
+            table = jnp.concatenate([out[j, h].reshape(512, 512) for j in range(4)], 1)
+            at = pl.ds(pl.multiple_of(SEQ * s, SEQ), SEQ)
             turned = dot_t(table, cotangent[at, :]).astype(bf16)
             wide_row = jnp.concatenate([turned[128 * g : 128 * g + 128] for g in range(4)], 1)
             spread = dot(wide_row, weights[h, s].reshape(1024, SEQ)).astype(bf16)
             back_value[at, pl.ds(128 * h, 128)] = spread.T
+            return carry
+
+        lax.fori_loop(0, 2, one, 0)
 
     def own_term(unit, zh, core):
         side = lax.rem(place.c + core, 2)
@@ -473,21 +475,17 @@
             copies.finish(early_only=True)
         left = normed_t if unit == 4 else context_t
 
-        def one(trip, carry):
-            for zh in range(2):
-                if unit == 4:
-                    right = back_value[:, pl.ds(256 * zh, 256)]
-                else:
-                    right = cotangent[:, pl.ds(512 * unit + 256 * zh, 256)]
-                both = dot(left[pl.ds(pl.multiple_of(1024 * trip, 1024), 1024), :], right).astype(bf16)
-                for core in range(2):
-                    h, lanes = own_term(unit, zh, core)
-                    qkv[h, pl.ds(2 * trip, 2), :, :, :, :, :, lanes] = both[
-                        :, 128 * core : 128 * core + 128
-                    ].reshape(2, 2, 4, 2, 2, 16, 128)
-            return carry
-
-        lax.fori_loop(0, 2, one, 0)
+        for zh in range(2):
+            if unit == 4:
+                right = back_value[:, pl.ds(256 * zh, 256)]
+            else:
+                right = cotangent[:, pl.ds(512 * unit + 256 * zh, 256)]
+            both = dot(left[...], right).astype(bf16)
+            for core in range(2):
+                h, lanes = own_term(unit, zh, core)
+                qkv[h, :, :, :, :, :, :, lanes] = both[:, 128 * core : 128 * core + 128].reshape(
+                    4, 2, 4, 2, 2, 16, 128
+                )
 
     def reduce_walk(which):
         unit, part_of, order = REDUCE_WALKS[which]
@@ -502,7 +500,7 @@
             qkv.at[source[0], :, :, :, every, :, :, pl.ds(source[1], 256)],
             theirs.at[unit, :, :, :, every],
             landing[3 * which : 3 * which + 3],
-            value_ref if unit == 4 else out_ref.at[:, pl.ds(128 * unit, 128)],
+            result.at[:, pl.ds(128 * unit, 128)],
             place,
             copies,
         )
@@ -553,12 +551,9 @@
     scratch += [(4, 512, 512), (512, 2048), (512, 512), (5, 4, 2, 4, 2, 2, 16, 256)] + landings
     return pl.pallas_call(
         whole_kernel,
-        out_shape=[
-            jax.ShapeDtypeStruct((64, 128), jnp.float32),
-            jax.ShapeDtypeStruct((64, 512), jnp.float32),
-        ],
+        out_shape=jax.ShapeDtypeStruct((64, 640), jnp.float32),
         in_specs=[pl.BlockSpec(memory_space=pltpu.SMEM)] + [vmem] * 2 + [anywhere] * 5,
-        out_specs=[vmem] * 2,
+        out_specs=vmem,
         scratch_shapes=[pltpu.VMEM(s, bf16) for s in scratch]
         + [
             pltpu.SemaphoreType.DMA((SENDS,)),
@@ -580,18 +575,17 @@
     ).astype(np.float32)
 
 def body(hidden, norm_gain, query_weight, key_weight, value_weight, output_weight, probe_seed):
-    return tuple(
-        whole(
-            probe_seed,
-            hidden,
-            norm_gain,
-            jnp.asarray(turn_tables()),
-            query_weight,
-            key_weight,
-            value_weight,
-            output_weight,
-        )
+    both = whole(
+        probe_seed,
+        hidden,
+        norm_gain,
+        jnp.asarray(turn_tables()),
+        query_weight,
+        key_weight,
+        value_weight,
+        output_weight,
     )
+    return both[:, 512:], both[:, :512]
 
 
 def solution(mesh):

time: 117 us -> 114 us (0.974)
  Pallas kernels: 113 us -> 109 us
    pallas_call x1, Pallas kernels: 113 us -> 109 us  [whole(): pl.pallas_call(whole_kernel, out_shape=jax.ShapeDtypeStruct((64, 640), jn...]
    slice x0 -> x2, local copies, waits for them, and re-layouts: none -> 2.94 us  [body(): return (both[:, 512:], both[:, :512])]
    unnamed x2 -> x0, local copies, waits for them, and re-layouts: 2.94 us -> none
where the time goes in v6:
time: 114 us; the launch traced here: 113 us
  Pallas kernels  109 us (96%)
  local copies, waits for them, and re-layouts  2.94 us (3%)
  between operations  1.29 us (1%)
    pallas_call x1, Pallas kernels, whole(): pl.pallas_call(whole_kernel, out_shape=jax.ShapeDtypeStruct((64, 640), jn...  109 us
    slice x2, local copies, waits for them, and re-layouts, body(): return (both[:, 512:], both[:, :512])  2.94 us

profile of v6, /device:TPU:0, one launch (start us, length us, event | category | flops | bytes accessed | tf_op | source)
XLA Modules:
  0.0 113.3 jit_solution(1567603074132728901)
XLA Ops:
  1.3 109.1 %shard_map.95 = f32[64,640]{1,0:T(8,128)} custom-call(s32[1]{0:T(128)S(6)} %copy.10.seed_ref, bf16[2048]{0:T(1024)(128)(2,1)} %gain.1, f32[2,256,128]{2,1,0:T(8,128)} %constant.2.clone.turns, bf16[512,2048]{1,0:T(8,128)(2,1)} %hidden.1, bf16[2,2,16,2048]{3,2,1,0:T(8,128)(2,1)} %bitcast.4, bf16[2,2,16,512]{3,2,1,0:T(8,128)(2,1)} %bitcast.6, ...), custom_call_target="tpu_custom_call" | custom-call | tf_op jit(solution)/shard_map/pallas_call | solution.py:552
  110.4 1.4 %slice.6 = f32[64,128]{1,0:T(8,128)} slice(f32[64,640]{1,0:T(8,128)} %shard_map.95), slice={[0:64], [512:640]} | slice | bytes 65536 | tf_op jit(solution)/shard_map/slice | solution.py:588
  111.7 1.6 %slice.7 = f32[64,512]{1,0:T(8,128)} slice(f32[64,640]{1,0:T(8,128)} %shard_map.95), slice={[0:64], [0:512]} | slice | bytes 262144 | tf_op jit(solution)/shard_map/slice | solution.py:588

commit v7 on v6

--- a/solution.py
+++ b/solution.py
@@ -574,6 +574,11 @@
         [np.concatenate([cosine, cosine], 1), np.concatenate([-sine, sine], 1)]
     ).astype(np.float32)
 
+def part_kernel(both, value_ref, out_ref):
+    value_ref[...] = both[:, 512:]
+    out_ref[...] = both[:, :512]
+
+
 def body(hidden, norm_gain, query_weight, key_weight, value_weight, output_weight, probe_seed):
     both = whole(
         probe_seed,
@@ -585,7 +590,15 @@
         value_weight,
         output_weight,
     )
-    return both[:, 512:], both[:, :512]
+    return tuple(
+        pl.pallas_call(
+            part_kernel,
+            out_shape=[
+                jax.ShapeDtypeStruct((64, 128), jnp.float32),
+                jax.ShapeDtypeStruct((64, 512), jnp.float32),
+            ],
+        )(both)
+    )
 
 
 def solution(mesh):

time: 114 us -> 112 us (0.982)
  local copies, waits for them, and re-layouts: 2.94 us -> 0 us
  Pallas kernels: 109 us -> 111 us
    slice x2 -> x0, local copies, waits for them, and re-layouts: 2.94 us -> none  [body(): return (both[:, 512:], both[:, :512])]
    pallas_call x0 -> x1, Pallas kernels: none -> 1.59 us  [body(): pl.pallas_call(part_kernel, out_shape=[jax.ShapeDtypeStruct((64, 128), jn...]
where the time goes in v7:
time: 112 us
  Pallas kernels  111 us (99%)
  between operations  1.29 us (1%)
    pallas_call x1, Pallas kernels, whole(): pl.pallas_call(whole_kernel, out_shape=jax.ShapeDtypeStruct((64, 640), jn...  109 us

profile of v7, /device:TPU:0, one launch (start us, length us, event | category | flops | bytes accessed | tf_op | source)
XLA Modules:
  0.0 111.9 jit_solution(14583975194935695002)
XLA Ops:
  1.3 109.1 %shard_map.95.both = f32[64,640]{1,0:T(8,128)} custom-call(s32[1]{0:T(128)S(6)} %copy.10.seed_ref, bf16[2048]{0:T(1024)(128)(2,1)} %gain.1, f32[2,256,128]{2,1,0:T(8,128)} %constant.2.clone.turns, bf16[512,2048]{1,0:T(8,128)(2,1)} %hidden.1, bf16[2,2,16,2048]{3,2,1,0:T(8,128)(2,1)} %bitcast.4, bf16[2,2,16,512]{3,2,1,0:T(8,128)(2,1)} %bitcast.6, ...), custom_call_target="tpu_custom_call" | custom-call | tf_op jit(solution)/shard_map/pallas_call | solution.py:552
  110.4 1.6 %shard_map.96 = (f32[64,128]{1,0:T(8,128)}, f32[64,512]{1,0:T(8,128)}) custom-call(f32[64,640]{1,0:T(8,128)} %shard_map.95.both), custom_call_target="tpu_custom_call" | custom-call | tf_op jit(solution)/shard_map/pallas_call | solution.py:594
